TPU v7x, 32 devices: a whole 2x2x4 slice. The times are simulated.
32 devices in a mesh: expert: 4 (over z), vocab: 2 (over x), batch: 4 (over y, core).
Axes of the slice: x: 2, y: 2, z: 4, core: 2. Of those that a mesh axis runs over, the one named last changes fastest.
Arguments:
- resid: bfloat16 [4, 64, 6144], P('batch', ('expert', 'vocab')), may hold values from -6 to 6
- moe_gain: float32 [6144], replicated, may hold values from 0.25 to 2.5
- final_gain: float32 [6144], replicated, may hold values from 0.5 to 1.5
- router: bfloat16 [6144, 4], replicated, may hold values from -0.078125 to 0.078125
- w_gate: bfloat16 [4, 6144, 8192], P('expert', None, ('vocab', 'batch')), may hold values from -0.078125 to 0.078125
- w_up: bfloat16 [4, 6144, 8192], P('expert', None, ('vocab', 'batch')), may hold values from -0.078125 to 0.078125
- w_down: bfloat16 [4, 8192, 6144], P('expert', ('vocab', 'batch')), may hold values from -0.0625 to 0.0625
- lm_head: bfloat16 [16384, 6144], P(('expert', 'vocab')), may hold values from -6 to 6
- expert_ids: int32 [4, 64, 2], P('batch', ('expert', 'vocab')), may hold values from 0 to 3, all different within a row; in each aligned block of 8 rows (0 to 7, 8 to 15, ..., all dimensions but the last counted through in order) at most 5 rows name the same one
- target_ids: int32 [4, 64], P('batch'), may hold values from 0 to 16383
- choice_len: int32 [4, 8], P('batch'), may hold values from 1 to 32, 64 in all within a row
- choice_question: int32 [4, 8], P('batch'), may hold values from 0 to 1, as said below
Outputs:
- token_logprob: float32 [4, 64], P('batch', ('expert', 'vocab'))
- choice_prob: float32 [4, 8], P('batch')
Inputs may be any that keep to these rules, and one draw needn't show every extreme that they name: `expert_ids`: A token's 2 experts differ; the rows of one device name each expert at most 5 times. `choice_len`: each group's lengths sum to 64. `choice_question`: in each group every question number appears exactly four times.
All inputs are finite; a program needn't handle non-finite values.
Results may differ from a plain program's by a relative error of at most 0.019.
Values may be sent and summed in bfloat16 or wider, within the bound.
A program may use at most 128 MiB of HBM per device.

v0:
```python
import functools

import jax
import jax.numpy as jnp
from jax import lax
from jax.experimental import pallas as pl
from jax.experimental.pallas import tpu as pltpu
from jax.sharding import PartitionSpec as P

epsilon = 1e-05


def joined(array, axis, combine):
    everything = jax.tree.map(lambda part: lax.all_gather(part, axis), array)
    leading = jax.tree.map(lambda part: part[0], everything)

    def lap(k, so_far):
        return combine(so_far, jax.tree.map(lambda part: part[k], everything))

    return lax.fori_loop(1, lax.axis_size(axis), lap, leading)


def rms_scale(values, gain):
    mean_square = jnp.mean(values * values, axis=-1, keepdims=True)
    return values * lax.rsqrt(mean_square + epsilon) * gain


def route_gates(router_logit, route_ids):
    expert_count = router_logit.shape[1]
    matches = route_ids[:, :, None] == jnp.arange(expert_count, dtype=jnp.int32)[None, None, :]
    picked = jnp.sum(jnp.where(matches, router_logit[:, None, :], 0.0), axis=2)
    return 1.0 / jnp.sum(jnp.exp(picked[:, None, :] - picked[:, :, None]), axis=2)


def expand_rows(block_rows, gate_cols, up_cols):
    gate_part = jnp.dot(block_rows, gate_cols, preferred_element_type=jnp.float32)
    up_part = jnp.dot(block_rows, up_cols, preferred_element_type=jnp.float32)
    return (jax.nn.silu(gate_part) * up_part).astype(jnp.bfloat16)


def choice_member(lengths, positions):
    ends = jnp.cumsum(lengths, dtype=jnp.int32)
    starts = ends - lengths
    return (positions[None, :] >= starts[:, None]) & (positions[None, :] < ends[:, None])


def choice_softmax(choice_total, lengths, questions):
    average = choice_total / lengths.astype(jnp.float32)
    same_question = questions[:, None] == questions[None, :]
    question_top = jnp.max(jnp.where(same_question, average[None, :], -jnp.inf), axis=1)
    raised = jnp.exp(average - question_top)
    denominator = jnp.sum(jnp.where(same_question, raised[None, :], 0.0), axis=1)
    return raised / denominator


def merge_stats(first, second):
    top_value = jnp.maximum(first[0], second[0])
    summed = first[1] * jnp.exp(first[0] - top_value) + second[1] * jnp.exp(second[0] - top_value)
    return (top_value, summed, first[2] + second[2])


def on_device(
    resid,
    moe_gain,
    final_gain,
    router,
    w_gate,
    w_up,
    w_down,
    lm_head,
    expert_ids,
    target_ids,
    choice_len,
    choice_question,
):
    stream = resid[0].astype(jnp.float32)
    token_count, model_width = stream.shape
    normed_in = rms_scale(stream, moe_gain).astype(jnp.bfloat16)
    router_logit = jnp.dot(normed_in, router, preferred_element_type=jnp.float32)
    route_ids = expert_ids[0]
    route_count = route_ids.shape[1]
    gate_weights = route_gates(router_logit, route_ids)
    expert_count = lax.axis_size("expert")
    bucket_size = max(2, (token_count * route_count + expert_count - 1) // expert_count + 1)
    flat_ids = route_ids.reshape(-1)
    expert_match = (flat_ids[:, None] == jnp.arange(expert_count, dtype=jnp.int32)[None, :]).astype(
        jnp.int32
    )
    earlier = jnp.cumsum(expert_match, axis=0, dtype=jnp.int32) - expert_match
    slot_index = flat_ids * bucket_size + jnp.sum(earlier * expert_match, axis=1)
    slot_match = (
        slot_index[:, None] == jnp.arange(expert_count * bucket_size, dtype=jnp.int32)[None, :]
    ).astype(jnp.float32)
    slot_match = slot_match.reshape(token_count, route_count, -1)
    dispatch = jnp.sum(slot_match, axis=1).astype(jnp.bfloat16)
    combine_weights = jnp.sum(slot_match * gate_weights[:, :, None], axis=1)
    buckets = lax.dot_general(
        dispatch, normed_in, (((0,), (0,)), ((), ())), preferred_element_type=jnp.float32
    )
    buckets = buckets.astype(jnp.bfloat16).reshape(expert_count, bucket_size, model_width)
    gate_cols = w_gate[0]
    up_cols = w_up[0]
    down_rows = w_down[0]
    arrived = lax.all_to_all(buckets, "expert", split_axis=0, concat_axis=0, tiled=True).reshape(
        -1, model_width
    )
    hidden = expand_rows(
        lax.all_gather(arrived, ("vocab", "batch"), axis=0, tiled=True), gate_cols, up_cols
    )
    expert_sum = lax.psum_scatter(
        jnp.dot(hidden, down_rows, preferred_element_type=jnp.float32).astype(jnp.bfloat16),
        ("vocab", "batch"),
        scatter_dimension=0,
        tiled=True,
    )
    outgoing = expert_sum.reshape(expert_count, bucket_size, model_width)
    returned = lax.all_to_all(outgoing, "expert", split_axis=0, concat_axis=0, tiled=True)
    returned_rows = returned.reshape(-1, model_width).astype(jnp.float32)
    mixed_rows = stream + jnp.dot(combine_weights, returned_rows, precision=lax.Precision.HIGHEST)
    normed_out = rms_scale(mixed_rows, final_gain).astype(jnp.bfloat16)
    head_index = lax.axis_index(("expert", "vocab"))
    vocab_share = lm_head.shape[0]
    vocab_ids = jnp.arange(vocab_share, dtype=jnp.int32) + head_index * vocab_share
    targets = target_ids[0]
    group_tokens = targets.shape[0]
    logits = lax.dot_general(
        lax.all_gather(normed_out, ("expert", "vocab"), axis=0, tiled=True),
        lm_head,
        (((1,), (1,)), ((), ())),
        preferred_element_type=jnp.float32,
    )
    block_top = jnp.max(logits, axis=1)
    block_sum = jnp.sum(jnp.exp(logits - block_top[:, None]), axis=1)
    block_hit = jnp.sum(jnp.where(targets[:, None] == vocab_ids[None, :], logits, 0.0), axis=1)
    fresh = (block_top, block_sum, block_hit)
    largest, spread_sum, chosen = tuple((fresh[slot] for slot in range(3)))
    lengths = choice_len[0]
    questions = choice_question[0]
    own_first = head_index * token_count
    group_positions = jnp.arange(group_tokens, dtype=jnp.int32)
    best, summed, target_sum = joined(
        (largest, spread_sum, chosen), ("expert", "vocab"), merge_stats
    )
    group_logprob = target_sum - (best + jnp.log(summed))
    choice_total = jnp.sum(
        jnp.where(choice_member(lengths, group_positions), group_logprob[None, :], 0.0), axis=1
    )
    own_logprob = lax.dynamic_slice_in_dim(group_logprob, own_first, token_count, 0)
    choice_prob = choice_softmax(choice_total, lengths, questions)
    return (own_logprob.reshape(1, -1), choice_prob.reshape(1, -1))


MESH = pl.DeviceIdType.MESH
VMEM_BYTES = 67043328
COLUMN_CHUNKS = 4


def greet(partners):
    barrier = pltpu.get_barrier_semaphore()
    for partner in partners:
        pl.semaphore_signal(barrier, inc=1, device_id=partner, device_id_type=MESH)
    pl.semaphore_wait(barrier, len(partners))


def push(src, dst, send_sem, recv_sem, partner):
    return pltpu.make_async_remote_copy(
        src_ref=src,
        dst_ref=dst,
        send_sem=send_sem,
        recv_sem=recv_sem,
        device_id=partner,
        device_id_type=MESH,
    )


def experts_kernel(
    ne,
    nv,
    nb,
    own_ref,
    resid_ref,
    gates_ref,
    gain_ref,
    wg_hbm,
    wu_hbm,
    wd_hbm,
    out_ref,
    wg,
    wu,
    wd,
    zin,
    xs,
    hid,
    part,
    rpair,
    rchip,
    zs,
    zo,
    w_sem,
    z_send,
    z_recv,
    c_send,
    c_recv,
    p_send,
    p_recv,
    rp_send,
    rp_recv,
    rc_send,
    rc_recv,
    rz_send,
    rz_recv,
):
    e, v, b = lax.axis_index("expert"), lax.axis_index("vocab"), lax.axis_index("batch")
    core = lax.rem(b, 2)
    other = 1 - core
    tokens, width = own_ref.shape
    block = ne * tokens
    chips = 4
    across = (e, 1 - v, b)
    along = (e, v, lax.rem(b + 2, 4))
    mate = (e, v, b + 1 - 2 * core)
    near = {1: along, 2: across}

    def at_expert(k):
        return (lax.rem(e + k, ne), v, b)

    loads = [
        pltpu.make_async_copy(src, dst, w_sem.at[i])
        for i, (src, dst) in enumerate(((wg_hbm.at[0], wg), (wu_hbm.at[0], wu), (wd_hbm.at[0], wd)))
    ]
    for load in loads:
        load.start()
    greet([at_expert(k) for k in range(1, ne)] + [across, along, mate])

    z_copies = [
        push(own_ref, zin.at[e], z_send.at[k], z_recv.at[k], at_expert(k)) for k in range(1, ne)
    ]
    for copy in z_copies:
        copy.start()
    zin[e] = own_ref[...]
    for copy in z_copies:
        copy.wait_recv()
    xs[0, core] = zin[...].astype(jnp.float32).reshape(block, width).astype(jnp.bfloat16)

    part_width = width // 2

    def piece(h):
        return pl.ds(h * part_width, part_width)

    def plane_push(src_slot, dst_slot, h, n):
        return push(
            xs.at[src_slot, core, :, piece(h)],
            xs.at[dst_slot, core, :, piece(h)],
            c_send.at[dst_slot, h],
            c_recv.at[dst_slot, h],
            near[n],
        )

    def mate_push(slot, h):
        return push(
            xs.at[slot, core, :, piece(h)],
            xs.at[slot, core, :, piece(h)],
            p_send.at[slot, h],
            p_recv.at[slot, h],
            mate,
        )

    c_copies = {(n, h): plane_push(0, n, h, n) for n in (1, 2) for h in (0, 1)}
    c_copies[3, 0] = plane_push(2, 3, 0, 1)
    c_copies[3, 1] = plane_push(1, 3, 1, 2)
    p_copies = {(slot, h): mate_push(slot, h) for slot in range(4) for h in (0, 1)}
    for key in ((2, 0), (1, 1), (2, 1), (1, 0)):
        c_copies[key].start()
    p_copies[0, 0].start()
    p_copies[0, 1].start()
    for key, follow in (((2, 0), (3, 0)), ((1, 1), (3, 1)), ((1, 0), None), ((2, 1), None)):
        c_copies[key].wait_recv()
        if follow is not None:
            c_copies[follow].start()
        p_copies[key].start()
    hidden_width = wg.shape[1]
    tile = min(256, hidden_width)
    rows = 2 * block

    def expand(first, count):
        @pl.loop(0, hidden_width // tile)
        def _(i):
            cols = pl.ds(pl.multiple_of(i * tile, tile), tile)
            x = xs[first : first + count].reshape(count * rows, width)
            g = jnp.dot(x, wg[:, cols], preferred_element_type=jnp.float32)
            u = jnp.dot(x, wu[:, cols], preferred_element_type=jnp.float32)
            hid[first * rows : (first + count) * rows, cols] = (
                g / (1.0 + jnp.exp(-g)) * u
            ).astype(jnp.bfloat16)

    loads[0].wait()
    loads[1].wait()
    for slot in (0, 1):
        for h in (0, 1):
            p_copies[slot, h].wait_recv()
    expand(0, 2)
    for h in (0, 1):
        c_copies[3, h].wait_recv()
        p_copies[3, h].start()
    for slot in (2, 3):
        for h in (0, 1):
            p_copies[slot, h].wait_recv()
    expand(2, 2)

    loads[2].wait()
    chunk = width // COLUMN_CHUNKS
    down_tile = 512 if chunk % 512 == 0 else 128
    rp, rd, rn, rz = {}, {}, {}, {}

    def columns(j):
        return pl.ds(j * chunk, chunk)

    def wide(ref_value):
        return ref_value.astype(jnp.float32)

    def down(j):
        @pl.loop(0, chunk // down_tile)
        def _(i):
            cols = pl.ds(pl.multiple_of(j * chunk + i * down_tile, down_tile), down_tile)
            y = jnp.dot(hid[...], wd[:, cols], preferred_element_type=jnp.float32)
            part[:, :, :, cols] = y.astype(jnp.bfloat16).reshape(chips, 2, block, down_tile)

        rp[j] = push(
            part.at[:, other, :, columns(j)],
            rpair.at[:, :, columns(j)],
            rp_send.at[j],
            rp_recv.at[j],
            mate,
        )
        rp[j].start()

    def neighbour_push(slot, j):
        return push(
            part.at[slot, core, :, columns(j)],
            rchip.at[slot - 1, :, columns(j)],
            rc_send.at[j, slot],
            rc_recv.at[j, slot],
            near[slot],
        )

    def pair_sum(j):
        rp[j].wait_recv()
        total = wide(part[:, core, :, columns(j)]) + wide(rpair[:, :, columns(j)])
        part[:, core, :, columns(j)] = total.astype(jnp.bfloat16)
        via = 2 - j % 2
        rd[j] = push(
            part.at[3, core, :, columns(j)],
            rchip.at[2, :, columns(j)],
            rc_send.at[j, 3],
            rc_recv.at[j, 3],
            near[via],
        )
        rd[j].start()
        rn[j, via] = neighbour_push(via, j)
        rn[j, via].start()

    def relay(j):
        last = 1 + j % 2
        rd[j].wait_recv()
        total = wide(part[last, core, :, columns(j)]) + wide(rchip[2, :, columns(j)])
        part[last, core, :, columns(j)] = total.astype(jnp.bfloat16)
        rn[j, last] = neighbour_push(last, j)
        rn[j, last].start()

    def plane_sum(j):
        rn[j, 1].wait_recv()
        rn[j, 2].wait_recv()
        total = wide(part[0, core, :, columns(j)])
        total = total + wide(rchip[0, :, columns(j)]) + wide(rchip[1, :, columns(j)])
        zs[:, :, columns(j)] = total.reshape(ne, tokens, chunk).astype(jnp.bfloat16)
        for k in range(1, ne):
            to = lax.rem(e + k, ne)
            rz[j, k] = push(
                zs.at[to, :, columns(j)],
                zo.at[e, :, columns(j)],
                rz_send.at[j, k],
                rz_recv.at[j, k],
                at_expert(k),
            )
            rz[j, k].start()
        zo[e, :, columns(j)] = zs[e, :, columns(j)]

    for j in range(COLUMN_CHUNKS):
        down(j)
        if j >= 1:
            pair_sum(j - 1)
    pair_sum(COLUMN_CHUNKS - 1)
    for j in range(COLUMN_CHUNKS):
        relay(j)
        if j >= 1:
            plane_sum(j - 1)
    plane_sum(COLUMN_CHUNKS - 1)
    for copy in rz.values():
        copy.wait_recv()
    gates = gates_ref[...]
    mixed = resid_ref[...].astype(jnp.float32)
    for k in range(ne):
        mixed = mixed + gates[:, k : k + 1] * zo[k].astype(jnp.float32)
    scale = lax.rsqrt(jnp.mean(mixed * mixed, axis=-1, keepdims=True) + epsilon)
    out_ref[...] = (mixed * scale * gain_ref[...]).astype(jnp.bfloat16)
    for group in (c_copies, p_copies, rp, rd, rn, rz):
        for copy in group.values():
            copy.wait_send()
    for copy in z_copies:
        copy.wait_send()


def experts_call(sizes, own, resid, gates, gain, w_gate, w_up, w_down):
    ne, nv, nb = sizes
    tokens, width = own.shape
    hidden_width = w_gate.shape[2]
    chips = nv * nb // 2
    block = ne * tokens
    bf16 = jnp.bfloat16
    dma = pltpu.SemaphoreType.DMA
    vm = pl.BlockSpec(memory_space=pltpu.VMEM)
    anywhere = pl.BlockSpec(memory_space=pl.ANY)
    n = COLUMN_CHUNKS
    return pl.pallas_call(
        functools.partial(experts_kernel, ne, nv, nb),
        out_shape=jax.ShapeDtypeStruct((tokens, width), bf16),
        in_specs=[vm, vm, vm, vm, anywhere, anywhere, anywhere],
        out_specs=vm,
        scratch_shapes=[
            pltpu.VMEM((width, hidden_width), bf16),
            pltpu.VMEM((width, hidden_width), bf16),
            pltpu.VMEM((hidden_width, width), bf16),
            pltpu.VMEM((ne, tokens, width), bf16),
            pltpu.VMEM((chips, 2, block, width), bf16),
            pltpu.VMEM((2 * chips * block, hidden_width), bf16),
            pltpu.VMEM((chips, 2, block, width), bf16),
            pltpu.VMEM((chips, block, width), bf16),
            pltpu.VMEM((max(1, chips - 1), block, width), bf16),
            pltpu.VMEM((ne, tokens, width), bf16),
            pltpu.VMEM((ne, tokens, width), bf16),
            dma((3,)),
            dma((ne,)),
            dma((ne,)),
            dma((chips, 2)),
            dma((chips, 2)),
            dma((chips, 2)),
            dma((chips, 2)),
            dma((n,)),
            dma((n,)),
            dma((n, chips)),
            dma((n, chips)),
            dma((n, ne)),
            dma((n, ne)),
        ],
        compiler_params=pltpu.CompilerParams(
            collective_id=0, has_side_effects=True, vmem_limit_bytes=VMEM_BYTES - 2 * 1024 * 1024
        ),
        name="experts",
    )(own, resid, gates, gain, w_gate, w_up, w_down)


def head_kernel(
    ne, nv, own_ref, target_ref, head_hbm, out_ref, head, ys, stats, h_sem, y_send, y_recv, s_send, s_recv
):
    e, v, b = lax.axis_index("expert"), lax.axis_index("vocab"), lax.axis_index("batch")
    peers = ne * nv
    me = e * nv + v
    share, width = head.shape
    tokens = own_ref.shape[0]
    rows = peers * tokens
    lanes = out_ref.shape[1]
    tile = min(256, share)

    def at(k):
        p = lax.rem(me + k, peers)
        return (p // nv, lax.rem(p, nv), b)

    parts = h_sem.shape[0]
    depth = share // parts
    loads = [
        pltpu.make_async_copy(
            head_hbm.at[pl.ds(i * depth, depth)], head.at[pl.ds(i * depth, depth)], h_sem.at[i]
        )
        for i in range(parts)
    ]
    for load in loads:
        load.start()
    greet([at(k) for k in range(1, peers)])
    across = (e, 1 - v, b)
    along = [
        push(own_ref, ys.at[me], y_send.at[0, k], y_recv.at[0, k], (lax.rem(e + k, ne), v, b))
        for k in range(1, ne)
    ]
    turns = [push(own_ref, ys.at[me], y_send.at[1, 0], y_recv.at[1, 0], across)]
    for k in range(1, ne):
        slot = lax.rem(e + ne - k, ne) * nv + v
        turns.append(push(ys.at[slot], ys.at[slot], y_send.at[1, k], y_recv.at[1, k], across))
    for copy in along:
        copy.start()
    turns[0].start()
    ys[me] = own_ref[...]
    for k in [1] + [k for k in range(ne - 1, 1, -1)]:
        along[k - 1].wait_recv()
        turns[k].start()
    for copy in turns:
        copy.wait_recv()
    copies = along + turns
    for load in loads:
        load.wait()
    y = ys[...].astype(jnp.float32).reshape(rows, width).astype(jnp.bfloat16)
    targets = target_ref[...]

    def lap(i, carry):
        top, total, hit = carry
        first = pl.multiple_of(i * tile, tile)
        logits = lax.dot_general(
            y,
            head[pl.ds(first, tile), :],
            (((1,), (1,)), ((), ())),
            preferred_element_type=jnp.float32,
        )
        ids = lax.broadcasted_iota(jnp.int32, logits.shape, 1) + (me * share + first)
        new_top = jnp.maximum(top, jnp.max(logits, axis=1, keepdims=True))
        total = total * jnp.exp(top - new_top) + jnp.sum(
            jnp.exp(logits - new_top), axis=1, keepdims=True
        )
        hit = hit + jnp.sum(jnp.where(ids == targets, logits, 0.0), axis=1, keepdims=True)
        return new_top, total, hit

    zero = jnp.zeros((rows, 1), jnp.float32)
    top, total, hit = lax.fori_loop(
        0, share // tile, lap, (jnp.full((rows, 1), -jnp.inf, jnp.float32), zero, zero)
    )
    eye = lax.broadcasted_iota(jnp.int32, (rows, lanes), 0) == lax.broadcasted_iota(
        jnp.int32, (rows, lanes), 1
    )

    def laid(column):
        return jnp.sum(jnp.where(eye, column, 0.0), axis=0, keepdims=True)

    line = lax.broadcasted_iota(jnp.int32, (8, lanes), 0)
    stats[me] = jnp.where(
        line == 0, laid(top), jnp.where(line == 1, laid(total), jnp.where(line == 2, laid(hit), 0.0))
    )
    sends = [
        push(stats.at[me], stats.at[me], s_send.at[k], s_recv.at[k], at(k)) for k in range(1, peers)
    ]
    for copy in sends:
        copy.start()
    for copy in sends:
        copy.wait_recv()
    every = stats[...]
    best = jnp.max(every[:, 0:1, :], axis=0)
    summed = jnp.sum(every[:, 1:2, :] * jnp.exp(every[:, 0:1, :] - best[None]), axis=0)
    chosen = jnp.sum(every[:, 2:3, :], axis=0)
    used = lax.broadcasted_iota(jnp.int32, (1, lanes), 1) < rows
    logprob = chosen - (best + jnp.log(jnp.where(used, summed, 1.0)))
    out_ref[...] = jnp.broadcast_to(logprob, out_ref.shape)
    for copy in copies + sends:
        copy.wait_send()


def head_call(sizes, own, targets, lm_head):
    ne, nv, nb = sizes
    tokens, width = own.shape
    peers = ne * nv
    dma = pltpu.SemaphoreType.DMA
    vm = pl.BlockSpec(memory_space=pltpu.VMEM)
    return pl.pallas_call(
        functools.partial(head_kernel, ne, nv),
        out_shape=jax.ShapeDtypeStruct((8, 128), jnp.float32),
        in_specs=[vm, vm, pl.BlockSpec(memory_space=pl.ANY)],
        out_specs=vm,
        scratch_shapes=[
            pltpu.VMEM(lm_head.shape, jnp.bfloat16),
            pltpu.VMEM((peers, tokens, width), jnp.bfloat16),
            pltpu.VMEM((peers, 8, 128), jnp.float32),
            dma((4,)),
            dma((2, ne)),
            dma((2, ne)),
            dma((peers,)),
            dma((peers,)),
        ],
        compiler_params=pltpu.CompilerParams(
            collective_id=1, has_side_effects=True, vmem_limit_bytes=VMEM_BYTES - 2 * 1024 * 1024
        ),
        name="head",
    )(own, targets, lm_head)


def kernels_fit(sizes, resid, w_gate, lm_head):
    ne, nv, nb = sizes
    tokens, width = resid.shape[1:]
    hidden_width = w_gate.shape[2]
    rows = ne * nv * nb * tokens
    need = 2 * (3 * width * hidden_width + rows * (3 * width + hidden_width) + 8 * ne * tokens * width)
    group = ne * nv * tokens
    head_need = 2 * (lm_head.shape[0] * width + 4 * group * width)
    return (
        nv == 2
        and nb == 4
        and tokens % 8 == 0
        and width % (128 * COLUMN_CHUNKS) == 0
        and hidden_width % 256 == 0
        and lm_head.shape[0] % 256 == 0
        and group <= 128
        and max(need, head_need) < VMEM_BYTES - 4 * 1024 * 1024
    )


def on_device_kernels(
    sizes,
    resid,
    moe_gain,
    final_gain,
    router,
    w_gate,
    w_up,
    w_down,
    lm_head,
    expert_ids,
    target_ids,
    choice_len,
    choice_question,
):
    ne, nv, nb = sizes
    stream = resid[0].astype(jnp.float32)
    token_count = stream.shape[0]
    normed_in = rms_scale(stream, moe_gain).astype(jnp.bfloat16)
    router_logit = jnp.dot(normed_in, router, preferred_element_type=jnp.float32)
    route_ids = expert_ids[0]
    gate_weights = route_gates(router_logit, route_ids)
    gates = jnp.sum(
        jnp.where(
            route_ids[:, :, None] == jnp.arange(ne, dtype=jnp.int32)[None, None, :],
            gate_weights[:, :, None],
            0.0,
        ),
        axis=1,
    )
    normed_out = experts_call(
        sizes, normed_in, resid[0], gates, final_gain.reshape(1, -1), w_gate, w_up, w_down
    )
    targets = target_ids[0]
    group_tokens = targets.shape[0]
    found = head_call(sizes, normed_out, targets.reshape(-1, 1), lm_head)
    group_logprob = found[0, :group_tokens]
    lengths = choice_len[0]
    positions = jnp.arange(group_tokens, dtype=jnp.int32)
    choice_total = jnp.sum(
        jnp.where(choice_member(lengths, positions), group_logprob[None, :], 0.0), axis=1
    )
    own_first = lax.axis_index(("expert", "vocab")) * token_count
    own_logprob = lax.dynamic_slice_in_dim(group_logprob, own_first, token_count, 0)
    choice_prob = choice_softmax(choice_total, lengths, choice_question[0])
    return (own_logprob.reshape(1, -1), choice_prob.reshape(1, -1))


def either(sizes, *arrays):
    if kernels_fit(sizes, arrays[0], arrays[4], arrays[7]):
        return on_device_kernels(sizes, *arrays)
    return on_device(*arrays)


def solution(mesh):
    sizes = tuple(mesh.shape[axis] for axis in ("expert", "vocab", "batch"))
    return jax.shard_map(
        functools.partial(either, sizes),
        mesh=mesh,
        in_specs=(
            P("batch", ("expert", "vocab"), None),
            P(),
            P(),
            P(),
            P("expert", None, ("vocab", "batch")),
            P("expert", None, ("vocab", "batch")),
            P("expert", ("vocab", "batch"), None),
            P(("expert", "vocab"), None),
            P("batch", ("expert", "vocab"), None),
            P("batch", None),
            P("batch", None),
            P("batch", None),
        ),
        out_specs=(P("batch", ("expert", "vocab")), P("batch", None)),
        check_vma=False,
    )
```

profile of v0, /device:TPU:0, one launch (start us, length us, event | category | flops | bytes accessed | tf_op | source)
XLA Modules:
  0.0 107.4 jit_solution(10771422433615355274)
XLA Ops:
  0.6 0.0 copy-start
  0.6 1.1 fusion
  1.7 1.0 fusion.2.own_ref
  2.7 0.0 copy-done
  2.7 0.0 copy-start.1
  2.8 0.2 fusion.8
  2.9 0.7 select_reduce_fusion.2
  3.7 0.7 select_reduce_fusion.1
  4.4 0.7 copy.17.gates_ref
  5.0 0.0 copy-done.1
  5.0 0.0 copy-start.3
  5.0 66.3 %experts.1.own_ref = bf16[8,6144]{1,0:T(8,128)(2,1)} custom-call(bf16[8,6144]{1,0:T(8,128)(2,1)} %copy-done.1, bf16[8,6144]{1,0:T(8,128)(2,1)} %bitcast.31, f32[8,4]{1,0:T(8,128)} %copy.17.gates_ref, f32[1,6144]{1,0:T(1,128)} %bitcast.32, bf16[1,6144,1024]{2,1,0:T(8,128)(2,1)} %wg_hbm.1, bf16[1,6144,1024]{2,1,0:T(8,128)(2,1)} %wu_hbm.1, ...), custom_call_target="tpu_custom_call" | custom-call | tf_op jit(solution)/shard_map/experts/pallas_call | solution.py:424
  71.3 0.0 copy-done.3
  71.3 0.7 copy.18.target_ref
  72.0 0.0 copy-start.4
  72.1 33.3 %head.1 = f32[8,128]{1,0:T(8,128)} custom-call(bf16[8,6144]{1,0:T(8,128)(2,1)} %experts.1.own_ref, s32[64,1]{1,0:T(8,128)} %copy.18.target_ref, bf16[2048,6144]{1,0:T(8,128)(2,1)} %head_hbm.1), custom_call_target="tpu_custom_call" | custom-call | tf_op jit(solution)/shard_map/head/pallas_call | solution.py:569
  105.4 0.7 slice_bitcast_fusion
  106.0 0.0 copy-done.4
  106.0 0.2 reduce-window.7
  106.2 0.2 select_reduce_fusion
  106.4 0.0 copy-done.2
  106.4 0.2 fusion.3
  106.6 0.2 fusion.4
  106.8 0.6 bitcast_divide_fusion
  (7 shorter events, 0.1 us)
Async XLA Ops:
  0.6 2.1 %copy-start = (bf16[6144,4]{0,1:T(4,128)(2,1)S(1)}, bf16[6144,4]{0,1:T(4,128)(2,1)}, u32[]{:S(2)}) copy-start(bf16[6144,4]{0,1:T(4,128)(2,1)} %param.15) | copy-start | bytes 147460
  2.7 2.3 %copy-start.1 = (bf16[8,6144]{1,0:T(8,128)(2,1)}, bf16[8,6144]{1,0:T(8,128)(2,1)S(1)}, u32[]{:S(2)}) copy-start(bf16[8,6144]{1,0:T(8,128)(2,1)S(1)} %fusion.2.own_ref) | copy-start | bytes 294916
  5.0 66.3 %copy-start.3 = (s32[1,64]{1,0:T(1,128)S(1)}, s32[1,64]{1,0:T(1,128)}, u32[]{:S(2)}) copy-start(s32[1,64]{1,0:T(1,128)} %param.21) | copy-start | bytes 772
  72.0 34.0 %copy-start.4 = (s32[1,8]{1,0:T(1,128)S(1)}, s32[1,8]{1,0:T(1,128)}, u32[]{:S(2)}) copy-start(s32[1,8]{1,0:T(1,128)} %param.22) | copy-start | bytes 100
  72.0 34.4 %copy-start.2 = (s32[1,8]{1,0:T(1,128)S(1)}, s32[1,8]{1,0:T(1,128)}, u32[]{:S(2)}) copy-start(s32[1,8]{1,0:T(1,128)} %param.23) | copy-start | bytes 100
where the time goes:
time: 108 us; the launch traced here: 107 us
  Pallas kernels  99.6 us (92%)
  other arithmetic  4.86 us (5%)
  local copies, waits for them, and re-layouts  2.06 us (2%)
    pallas_call x1, Pallas kernels, experts_call(): pl.pallas_call(functools.partial(experts_kernel, ne, nv, nb), out_shape=j...  66.3 us
    pallas_call x1, Pallas kernels, head_call(): pl.pallas_call(functools.partial(head_kernel, ne, nv), out_shape=jax.Shap...  33.3 us

commit v1 on v0

v1 whole, which is shorter than its diff:
```python
import functools

import jax
import jax.numpy as jnp
from jax import lax
from jax.experimental import pallas as pl
from jax.experimental.pallas import tpu as pltpu
from jax.sharding import PartitionSpec as P

epsilon = 1e-05


def joined(array, axis, combine):
    everything = jax.tree.map(lambda part: lax.all_gather(part, axis), array)
    leading = jax.tree.map(lambda part: part[0], everything)

    def lap(k, so_far):
        return combine(so_far, jax.tree.map(lambda part: part[k], everything))

    return lax.fori_loop(1, lax.axis_size(axis), lap, leading)


def rms_scale(values, gain):
    mean_square = jnp.mean(values * values, axis=-1, keepdims=True)
    return values * lax.rsqrt(mean_square + epsilon) * gain


def route_gates(router_logit, route_ids):
    expert_count = router_logit.shape[1]
    matches = route_ids[:, :, None] == jnp.arange(expert_count, dtype=jnp.int32)[None, None, :]
    picked = jnp.sum(jnp.where(matches, router_logit[:, None, :], 0.0), axis=2)
    return 1.0 / jnp.sum(jnp.exp(picked[:, None, :] - picked[:, :, None]), axis=2)


def expand_rows(block_rows, gate_cols, up_cols):
    gate_part = jnp.dot(block_rows, gate_cols, preferred_element_type=jnp.float32)
    up_part = jnp.dot(block_rows, up_cols, preferred_element_type=jnp.float32)
    return (jax.nn.silu(gate_part) * up_part).astype(jnp.bfloat16)


def choice_member(lengths, positions):
    ends = jnp.cumsum(lengths, dtype=jnp.int32)
    starts = ends - lengths
    return (positions[None, :] >= starts[:, None]) & (positions[None, :] < ends[:, None])


def choice_softmax(choice_total, lengths, questions):
    average = choice_total / lengths.astype(jnp.float32)
    same_question = questions[:, None] == questions[None, :]
    question_top = jnp.max(jnp.where(same_question, average[None, :], -jnp.inf), axis=1)
    raised = jnp.exp(average - question_top)
    denominator = jnp.sum(jnp.where(same_question, raised[None, :], 0.0), axis=1)
    return raised / denominator


def merge_stats(first, second):
    top_value = jnp.maximum(first[0], second[0])
    summed = first[1] * jnp.exp(first[0] - top_value) + second[1] * jnp.exp(second[0] - top_value)
    return (top_value, summed, first[2] + second[2])


def on_device(
    resid,
    moe_gain,
    final_gain,
    router,
    w_gate,
    w_up,
    w_down,
    lm_head,
    expert_ids,
    target_ids,
    choice_len,
    choice_question,
):
    stream = resid[0].astype(jnp.float32)
    token_count, model_width = stream.shape
    normed_in = rms_scale(stream, moe_gain).astype(jnp.bfloat16)
    router_logit = jnp.dot(normed_in, router, preferred_element_type=jnp.float32)
    route_ids = expert_ids[0]
    route_count = route_ids.shape[1]
    gate_weights = route_gates(router_logit, route_ids)
    expert_count = lax.axis_size("expert")
    bucket_size = max(2, (token_count * route_count + expert_count - 1) // expert_count + 1)
    flat_ids = route_ids.reshape(-1)
    expert_match = (flat_ids[:, None] == jnp.arange(expert_count, dtype=jnp.int32)[None, :]).astype(
        jnp.int32
    )
    earlier = jnp.cumsum(expert_match, axis=0, dtype=jnp.int32) - expert_match
    slot_index = flat_ids * bucket_size + jnp.sum(earlier * expert_match, axis=1)
    slot_match = (
        slot_index[:, None] == jnp.arange(expert_count * bucket_size, dtype=jnp.int32)[None, :]
    ).astype(jnp.float32)
    slot_match = slot_match.reshape(token_count, route_count, -1)
    dispatch = jnp.sum(slot_match, axis=1).astype(jnp.bfloat16)
    combine_weights = jnp.sum(slot_match * gate_weights[:, :, None], axis=1)
    buckets = lax.dot_general(
        dispatch, normed_in, (((0,), (0,)), ((), ())), preferred_element_type=jnp.float32
    )
    buckets = buckets.astype(jnp.bfloat16).reshape(expert_count, bucket_size, model_width)
    gate_cols = w_gate[0]
    up_cols = w_up[0]
    down_rows = w_down[0]
    arrived = lax.all_to_all(buckets, "expert", split_axis=0, concat_axis=0, tiled=True).reshape(
        -1, model_width
    )
    hidden = expand_rows(
        lax.all_gather(arrived, ("vocab", "batch"), axis=0, tiled=True), gate_cols, up_cols
    )
    expert_sum = lax.psum_scatter(
        jnp.dot(hidden, down_rows, preferred_element_type=jnp.float32).astype(jnp.bfloat16),
        ("vocab", "batch"),
        scatter_dimension=0,
        tiled=True,
    )
    outgoing = expert_sum.reshape(expert_count, bucket_size, model_width)
    returned = lax.all_to_all(outgoing, "expert", split_axis=0, concat_axis=0, tiled=True)
    returned_rows = returned.reshape(-1, model_width).astype(jnp.float32)
    mixed_rows = stream + jnp.dot(combine_weights, returned_rows, precision=lax.Precision.HIGHEST)
    normed_out = rms_scale(mixed_rows, final_gain).astype(jnp.bfloat16)
    head_index = lax.axis_index(("expert", "vocab"))
    vocab_share = lm_head.shape[0]
    vocab_ids = jnp.arange(vocab_share, dtype=jnp.int32) + head_index * vocab_share
    targets = target_ids[0]
    group_tokens = targets.shape[0]
    logits = lax.dot_general(
        lax.all_gather(normed_out, ("expert", "vocab"), axis=0, tiled=True),
        lm_head,
        (((1,), (1,)), ((), ())),
        preferred_element_type=jnp.float32,
    )
    block_top = jnp.max(logits, axis=1)
    block_sum = jnp.sum(jnp.exp(logits - block_top[:, None]), axis=1)
    block_hit = jnp.sum(jnp.where(targets[:, None] == vocab_ids[None, :], logits, 0.0), axis=1)
    fresh = (block_top, block_sum, block_hit)
    largest, spread_sum, chosen = tuple((fresh[slot] for slot in range(3)))
    lengths = choice_len[0]
    questions = choice_question[0]
    own_first = head_index * token_count
    group_positions = jnp.arange(group_tokens, dtype=jnp.int32)
    best, summed, target_sum = joined(
        (largest, spread_sum, chosen), ("expert", "vocab"), merge_stats
    )
    group_logprob = target_sum - (best + jnp.log(summed))
    choice_total = jnp.sum(
        jnp.where(choice_member(lengths, group_positions), group_logprob[None, :], 0.0), axis=1
    )
    own_logprob = lax.dynamic_slice_in_dim(group_logprob, own_first, token_count, 0)
    choice_prob = choice_softmax(choice_total, lengths, questions)
    return (own_logprob.reshape(1, -1), choice_prob.reshape(1, -1))


MESH = pl.DeviceIdType.MESH
VMEM_BYTES = 67043328
CHUNKS = 6


def greet(partners):
    barrier = pltpu.get_barrier_semaphore()
    for partner in partners:
        pl.semaphore_signal(barrier, inc=1, device_id=partner, device_id_type=MESH)
    pl.semaphore_wait(barrier, len(partners))


def push(src, dst, send_sem, recv_sem, partner):
    return pltpu.make_async_remote_copy(
        src_ref=src,
        dst_ref=dst,
        send_sem=send_sem,
        recv_sem=recv_sem,
        device_id=partner,
        device_id_type=MESH,
    )


SKEW_MIX = 5
SKEW_FORWARD = 7
SKEW_HEAD = 8


def row_cap(ne, tokens, routes):
    return max(2, (tokens * routes + ne - 1) // ne + 1)


def wide(value):
    return value.astype(jnp.float32)


def iota(shape, axis):
    return lax.broadcasted_iota(jnp.int32, shape, axis)


def as_column(row, count):
    eye = iota((count, row.shape[1]), 0) == iota((count, row.shape[1]), 1)
    return jnp.sum(jnp.where(eye, row, 0.0), axis=1, keepdims=True)


def as_row(column, lanes):
    count = column.shape[0]
    eye = iota((count, lanes), 0) == iota((count, lanes), 1)
    return jnp.sum(jnp.where(eye, column, 0.0), axis=0, keepdims=True)


def fused_kernel(
    ne,
    nv,
    nb,
    cap,
    resid_ref,
    moe_gain_ref,
    final_gain_ref,
    router_ref,
    ids_ref,
    target_ref,
    length_ref,
    question_ref,
    wg_hbm,
    wu_hbm,
    wd_hbm,
    head_hbm,
    logprob_ref,
    prob_ref,
    big,
    wd,
    zout,
    zin,
    xs,
    xl,
    g_acc,
    u_acc,
    hid,
    pm,
    po,
    rpair,
    sy,
    ry,
    sx,
    rx,
    zs,
    zo,
    ys,
    logits,
    scales,
    stats,
    w_sem,
    wd_sem,
    h_sem,
    z_send,
    z_recv,
    c_send,
    c_recv,
    m_send,
    m_recv,
    r_send,
    r_recv,
    o_send,
    o_recv,
    y_send,
    y_recv,
    s_send,
    s_recv,
):
    e, v, b = lax.axis_index("expert"), lax.axis_index("vocab"), lax.axis_index("batch")
    core = lax.rem(b, 2)
    other = 1 - core
    tokens, width = resid_ref.shape
    half = width // 2
    n = CHUNKS
    cw = half // n
    chip_rows = ne * 2 * cap
    tiles = chip_rows // 8
    rows = 4 * chip_rows
    hidden = hid.shape[1]
    share = head_hbm.shape[0]
    block = big.shape[1]
    peers = ne * nv
    me = e * nv + v
    across = (e, 1 - v, b)
    along = (e, v, lax.rem(b + 2, 4))
    turned = b + 1 - 2 * core
    mate = (e, v, turned)
    bf16 = jnp.bfloat16

    def cols(j):
        return pl.ds(j * cw, cw)

    column = []
    for k in range(ne):
        for s in range(2):
            if k + s > 0:
                to = lax.rem(e + k, ne)
                column.append((k * 2 + s, to, other if s else core, (to, v, turned if s else b)))

    def at(k):
        p = lax.rem(me + k, peers)
        return (p // nv, lax.rem(p, nv), b)

    weight_loads = {}
    for j in range(n):
        for which, source in enumerate((wg_hbm, wu_hbm)):
            for h in range(2):
                first = h * half + j * cw
                weight_loads[j, which, h] = pltpu.make_async_copy(
                    source.at[0, pl.ds(first, cw)],
                    big.at[pl.ds(which * width + first, cw)],
                    w_sem.at[j, which * 2 + h],
                )
                weight_loads[j, which, h].start()
    down_load = pltpu.make_async_copy(wd_hbm.at[0], wd, wd_sem.at[0])
    down_load.start()

    barrier = pltpu.get_barrier_semaphore()
    greeted = [where for _, _, _, where in column]
    greeted += [(lax.rem(e + k, ne), 1 - v, b) for k in range(ne)] + [along]
    for partner in greeted:
        pl.semaphore_signal(barrier, inc=1, device_id=partner, device_id_type=MESH)

    stream = wide(resid_ref[...])
    mean_square = jnp.sum(stream * stream, axis=1, keepdims=True) * (1.0 / width)
    normed = wide((stream * lax.rsqrt(mean_square + epsilon) * moe_gain_ref[...]).astype(bf16))
    ids = wide(ids_ref[...])
    first_row, second_row = ids[0:1, :], ids[1:2, :]
    expert_of = wide(lax.shift_right_logical(iota((ne * 8, tokens), 0), 3))
    slot_of = wide(iota((ne * 8, tokens), 0) & 7)
    named = (first_row == expert_of) | (second_row == expert_of)
    before = jnp.where(iota((tokens, tokens), 0) < iota((tokens, tokens), 1), 1.0, 0.0)
    rank = jnp.dot(jnp.where(named, 1.0, 0.0), before, preferred_element_type=jnp.float32)
    dispatch = jnp.where(named & (rank == slot_of), 1.0, 0.0)
    for h in range(2):
        for j in range(n):
            first = h * half + j * cw
            routed = jnp.dot(
                dispatch, normed[:, first : first + cw], preferred_element_type=jnp.float32
            )
            zout[h, :, :, cols(j)] = routed.reshape(ne, 8, cw).astype(bf16)
    pl.semaphore_wait(barrier, len(greeted))

    z_copies = {}
    for j in range(n):
        for slot, to, ct, where in column:
            z_copies[j, slot] = push(
                zout.at[ct, to, :, cols(j)],
                zin.at[e, core, :, cols(j)],
                z_send.at[j, slot],
                z_recv.at[j, slot],
                where,
            )
            z_copies[j, slot].start()
    zin[e, core] = zout[core, e]

    first_id, second_id = as_column(first_row, tokens), as_column(second_row, tokens)
    expert_lane = wide(lax.shift_right_logical(iota((tokens, ne * 8), 1), 3))
    slot_lane = wide(iota((tokens, ne * 8), 1) & 7)
    first_here, second_here = first_id == expert_lane, second_id == expert_lane
    after = jnp.where(iota((tokens, tokens), 1) < iota((tokens, tokens), 0), 1.0, 0.0)
    rank = jnp.dot(
        after, jnp.where(first_here | second_here, 1.0, 0.0), preferred_element_type=jnp.float32
    )
    first_logit = jnp.zeros((tokens, 1), jnp.float32)
    second_logit = jnp.zeros((tokens, 1), jnp.float32)
    for k in range(ne):
        router_logit = jnp.sum(normed * wide(router_ref[k : k + 1, :]), axis=1, keepdims=True)
        first_logit = first_logit + jnp.where(first_id == k, router_logit, 0.0)
        second_logit = second_logit + jnp.where(second_id == k, router_logit, 0.0)
    first_gate = 1.0 / (1.0 + jnp.exp(second_logit - first_logit))
    second_gate = 1.0 / (1.0 + jnp.exp(first_logit - second_logit))
    combine = jnp.where(
        rank == slot_lane,
        jnp.where(first_here, first_gate, jnp.where(second_here, second_gate, 0.0)),
        0.0,
    )
    coarse = wide(combine.astype(bf16))
    combine = jnp.concatenate([coarse, combine - coarse], axis=0).astype(bf16)

    def packing(shape, packed_axis):
        padded = iota(shape, 1 - packed_axis)
        slot = padded & 7
        place = lax.shift_right_logical(padded, 3) * cap + slot
        return jnp.where((slot < cap) & (place == iota(shape, packed_axis)), 1.0, 0.0).astype(bf16)

    pack = packing((chip_rows, ne * 16), 0)
    unpack = packing((ne * 16, chip_rows), 1)

    def plane_push(src_slot, dst_slot, j, partner):
        return push(
            xs.at[src_slot, core, :, :, cols(j)],
            xs.at[dst_slot, core, :, :, cols(j)],
            c_send.at[j, dst_slot],
            c_recv.at[j, dst_slot],
            partner,
        )

    c_copies, m_copies = {}, {}

    def mate_push(slot, j):
        m_copies[j, slot] = push(
            xs.at[slot, core, :, :, cols(j)],
            xs.at[slot, core, :, :, cols(j)],
            m_send.at[j, slot],
            m_recv.at[j, slot],
            mate,
        )
        m_copies[j, slot].start()

    def pack_rows(j):
        for slot, _, _, _ in column:
            z_copies[j, slot].wait_recv()
        padded = wide(zin[:, :, :, cols(j)]).reshape(ne * 16, cw).astype(bf16)
        packed = jnp.dot(pack, padded, preferred_element_type=jnp.float32)
        xs[0, core, :, :, cols(j)] = packed.reshape(tiles, 8, cw).astype(bf16)
        for slot, partner in ((1, across), (2, along)):
            c_copies[j, slot] = plane_push(0, slot, j, partner)
            c_copies[j, slot].start()
        mate_push(0, j)

    def relay(j):
        source, partner = (1, along) if j % 2 == 0 else (2, across)
        c_copies[j, source].wait_recv()
        c_copies[j, 3] = plane_push(source, 3, j, partner)
        c_copies[j, 3].start()
        mate_push(source, j)
        c_copies[j, 3 - source].wait_recv()
        mate_push(3 - source, j)

    def corner(j):
        c_copies[j, 3].wait_recv()
        mate_push(3, j)

    tile = min(256, hidden)

    def expand(j):
        for slot in range(4):
            m_copies[j, slot].wait_recv()
        for h in range(2):
            xl[h] = wide(xs[:, h, :, :, cols(j)]).reshape(rows, cw).astype(bf16)
        for which in range(2):
            for h in range(2):
                weight_loads[j, which, h].wait()

        @pl.loop(0, hidden // tile)
        def _(i):
            where = pl.ds(pl.multiple_of(i * tile, tile), tile)

            def product(which):
                low = which * width + j * cw
                return jnp.dot(
                    xl[0], big[low : low + cw, where], preferred_element_type=jnp.float32
                ) + jnp.dot(
                    xl[1],
                    big[low + half : low + half + cw, where],
                    preferred_element_type=jnp.float32,
                )

            g, u = product(0), product(1)
            if j > 0:
                g, u = g + g_acc[:, where], u + u_acc[:, where]
            if j < n - 1:
                g_acc[:, where] = g
                u_acc[:, where] = u
            else:
                hid[:, where] = (g / (1.0 + jnp.exp(-g)) * u).astype(bf16)

    for i in range(n + 3):
        for skew, stage in enumerate((pack_rows, relay, corner, expand)):
            if 0 <= i - skew < n:
                stage(i - skew)

    head_loads = []
    per_half = half // block
    for q in range(per_half):
        for h in range(2):
            place = h * per_half + q
            head_loads.append(
                pltpu.make_async_copy(
                    head_hbm.at[:, pl.ds(place * block, block)],
                    big.at[pl.ds(place * share, share)],
                    h_sem.at[place],
                )
            )
            head_loads[-1].start()
    down_load.wait()

    rp, yc, xc, zc, gz, gx = {}, {}, {}, {}, {}, {}

    def down(j):
        def product(side):
            where = pl.ds(pl.multiple_of(side * half + j * cw, 128), cw)
            return jnp.dot(hid[...], wd[:, where], preferred_element_type=jnp.float32)

        pm[:, :, :, cols(j)] = product(other).reshape(4, tiles, 8, cw).astype(bf16)
        rp[j] = push(
            pm.at[:, :, :, cols(j)], rpair.at[:, :, :, cols(j)], r_send.at[j, 0], r_recv.at[j, 0], mate
        )
        rp[j].start()
        po[:, cols(j)] = product(core)

    def pair_sum(j):
        rp[j].wait_recv()
        total = po[:, cols(j)] + wide(rpair[:, :, :, cols(j)]).reshape(rows, cw)
        sy[:, :, :, cols(j)] = total[2 * chip_rows :].reshape(2, tiles, 8, cw).astype(bf16)
        yc[j] = push(
            sy.at[:, :, :, cols(j)], ry.at[:, :, :, cols(j)], r_send.at[j, 1], r_recv.at[j, 1], along
        )
        yc[j].start()
        po[0 : 2 * chip_rows, cols(j)] = total[: 2 * chip_rows]

    def y_sum(j):
        yc[j].wait_recv()
        total = po[0 : 2 * chip_rows, cols(j)] + wide(ry[:, :, :, cols(j)]).reshape(2 * chip_rows, cw)
        sx[:, :, cols(j)] = total[chip_rows:].reshape(tiles, 8, cw).astype(bf16)
        xc[j] = push(
            sx.at[:, :, cols(j)], rx.at[:, :, cols(j)], r_send.at[j, 2], r_recv.at[j, 2], across
        )
        xc[j].start()
        po[0:chip_rows, cols(j)] = total[:chip_rows]

    def x_sum(j):
        xc[j].wait_recv()
        total = po[0:chip_rows, cols(j)] + wide(rx[:, :, cols(j)]).reshape(chip_rows, cw)
        padded = jnp.dot(unpack, total.astype(bf16), preferred_element_type=jnp.float32)
        zs[:, :, :, cols(j)] = padded.reshape(ne, 2, 8, cw).astype(bf16)
        for slot, to, ct, where in column:
            zc[j, slot] = push(
                zs.at[to, ct, :, cols(j)],
                zo.at[e, core, :, cols(j)],
                o_send.at[j, slot],
                o_recv.at[j, slot],
                where,
            )
            zc[j, slot].start()
        zo[e, core, :, cols(j)] = zs[e, core, :, cols(j)]

    squares = [jnp.zeros((tokens, 1), jnp.float32)]

    def mix(j):
        for slot, _, _, _ in column:
            zc[j, slot].wait_recv()
        for h in range(2):
            first = h * half + j * cw
            returned = wide(zo[:, h, :, cols(j)]).reshape(ne * 8, cw).astype(bf16)
            weighted = jnp.dot(combine, returned, preferred_element_type=jnp.float32)
            mixed = wide(resid_ref[:, first : first + cw]) + (weighted[:tokens] + weighted[tokens:])
            squares[0] = squares[0] + jnp.sum(mixed * mixed, axis=1, keepdims=True)
            ys[me, j, h] = (mixed * final_gain_ref[:, first : first + cw]).astype(bf16)
        for k in range(1, ne):
            gz[j, k] = push(
                ys.at[me, j],
                ys.at[me, j],
                y_send.at[j, k],
                y_recv.at[j, k],
                (lax.rem(e + k, ne), v, b),
            )
            gz[j, k].start()
        turn(j, 0)

    def turn(j, k):
        slot = lax.rem(e + ne - k, ne) * nv + v
        gx[j, k] = push(
            ys.at[slot, j], ys.at[slot, j], y_send.at[j, ne + k], y_recv.at[j, ne + k], across
        )
        gx[j, k].start()

    def forward(j):
        for k in (1, 3, 2) if ne == 4 else range(1, ne):
            gz[j, k].wait_recv()
            turn(j, k)

    head_tile = min(256, share)

    def head(j):
        for k in range(ne):
            gx[j, k].wait_recv()
        if (j * cw) % block == 0:
            for h in range(2):
                head_loads[(j * cw) // block * 2 + h].wait()
        sides = []
        for h in range(2):
            sides.append(wide(ys[:, j, h]).reshape(peers * tokens, cw).astype(bf16))
        left = (j * cw) % block
        low = (j * cw) // block * share

        @pl.loop(0, share // head_tile)
        def _(i):
            first = pl.multiple_of(i * head_tile, head_tile)
            found = 0.0
            for h in range(2):
                found = found + lax.dot_general(
                    sides[h],
                    big[pl.ds(low + h * per_half * share + first, head_tile), left : left + cw],
                    (((1,), (1,)), ((), ())),
                    preferred_element_type=jnp.float32,
                )
            if j > 0:
                found = found + logits[:, pl.ds(first, head_tile)]
            logits[:, pl.ds(first, head_tile)] = found

    small = []

    def share_scale(j):
        if j < n - 1:
            return
        scale = lax.rsqrt(squares[0] * (1.0 / width) + epsilon)
        scales[me] = jnp.broadcast_to(scale, (tokens, 128))
        for k in range(1, peers):
            small.append(
                push(scales.at[me], scales.at[me], s_send.at[0, k], s_recv.at[0, k], at(k))
            )
            small[-1].start()

    stages = (
        (0, down),
        (1, pair_sum),
        (2, y_sum),
        (3, x_sum),
        (SKEW_MIX, mix),
        (SKEW_MIX, share_scale),
        (SKEW_FORWARD, forward),
        (SKEW_HEAD, head),
    )
    for i in range(n + SKEW_HEAD):
        for skew, stage in stages:
            if 0 <= i - skew < n:
                stage(i - skew)

    for copy in small:
        copy.wait_recv()
    group = peers * tokens
    lanes = 128
    scaled = logits[...] * scales[...].reshape(group, lanes)[:, 0:1]
    targets = as_column(wide(target_ref[...]), group)
    vocab_ids = wide(iota((group, share), 1) + me * share)
    top = jnp.max(scaled, axis=1, keepdims=True)
    total = jnp.sum(jnp.exp(scaled - top), axis=1, keepdims=True)
    hit = jnp.sum(jnp.where(vocab_ids == targets, scaled, 0.0), axis=1, keepdims=True)
    line = iota((8, lanes), 0)
    stats[me] = jnp.where(
        line == 0,
        as_row(top, lanes),
        jnp.where(line == 1, as_row(total, lanes), jnp.where(line == 2, as_row(hit, lanes), 0.0)),
    )
    sends = [
        push(stats.at[me], stats.at[me], s_send.at[1, k], s_recv.at[1, k], at(k))
        for k in range(1, peers)
    ]
    for copy in sends:
        copy.start()

    choices = length_ref.shape[1]
    lengths_row, questions_row = wide(length_ref[...]), wide(question_ref[...])
    lengths, questions = as_column(lengths_row, choices), as_column(questions_row, choices)
    square = (choices, choices)
    ends = jnp.sum(jnp.where(iota(square, 1) <= iota(square, 0), lengths_row, 0.0), axis=1, keepdims=True)
    place = wide(iota((choices, lanes), 1))
    member = (place >= ends - lengths) & (place < ends)
    same = questions == questions_row

    for copy in sends:
        copy.wait_recv()
    every = stats[...]
    best = jnp.max(every[:, 0:1, :], axis=0)
    summed = jnp.sum(every[:, 1:2, :] * jnp.exp(every[:, 0:1, :] - best[None]), axis=0)
    chosen = jnp.sum(every[:, 2:3, :], axis=0)
    used = iota((1, lanes), 1) < group
    logprob = jnp.where(used, chosen - (best + jnp.log(jnp.where(used, summed, 1.0))), 0.0)
    own = jnp.sum(
        jnp.where(iota((tokens, lanes), 1) == iota((tokens, lanes), 0) + me * tokens, logprob, 0.0),
        axis=1,
        keepdims=True,
    )
    logprob_ref[...] = as_row(own, tokens)
    average = jnp.sum(jnp.where(member, logprob, 0.0), axis=1, keepdims=True) / lengths
    question_top = jnp.max(
        jnp.where(same, as_row(average, choices), -jnp.inf), axis=1, keepdims=True
    )
    raised = jnp.exp(average - question_top)
    denominator = jnp.sum(jnp.where(same, as_row(raised, choices), 0.0), axis=1, keepdims=True)
    prob_ref[...] = as_row(raised / denominator, choices)

    for copies in (z_copies, c_copies, m_copies, rp, yc, xc, zc, gz, gx):
        for copy in copies.values():
            copy.wait_send()
    for copy in small + sends:
        copy.wait_send()


def fused_call(sizes, resid, moe_gain, final_gain, router, ids, targets, lengths, questions, *weights):
    ne, nv, nb = sizes
    tokens, width = resid.shape
    w_gate, _, _, lm_head = weights
    hidden = w_gate.shape[2]
    share = lm_head.shape[0]
    cap = row_cap(ne, tokens, ids.shape[0])
    half = width // 2
    tiles = ne * 2 * cap // 8
    rows = 4 * tiles * 8
    peers = ne * nv
    n = CHUNKS
    cw = half // n
    bf16, f32 = jnp.bfloat16, jnp.float32
    dma = pltpu.SemaphoreType.DMA
    vmem = pltpu.VMEM
    vm = pl.BlockSpec(memory_space=pltpu.VMEM)
    anywhere = pl.BlockSpec(memory_space=pl.ANY)
    return pl.pallas_call(
        functools.partial(fused_kernel, ne, nv, nb, cap),
        out_shape=(
            jax.ShapeDtypeStruct((1, tokens), f32),
            jax.ShapeDtypeStruct((1, lengths.shape[1]), f32),
        ),
        in_specs=[vm] * 8 + [anywhere] * 4,
        out_specs=(vm, vm),
        scratch_shapes=[
            vmem((2 * width, hidden), bf16),
            vmem((hidden, width), bf16),
            vmem((2, ne, 8, half), bf16),
            vmem((ne, 2, 8, half), bf16),
            vmem((4, 2, tiles, 8, half), bf16),
            vmem((2, rows, cw), bf16),
            vmem((rows, hidden), f32),
            vmem((rows, hidden), f32),
            vmem((rows, hidden), bf16),
            vmem((4, tiles, 8, half), bf16),
            vmem((rows, half), f32),
            vmem((4, tiles, 8, half), bf16),
            vmem((2, tiles, 8, half), bf16),
            vmem((2, tiles, 8, half), bf16),
            vmem((tiles, 8, half), bf16),
            vmem((tiles, 8, half), bf16),
            vmem((ne, 2, 8, half), bf16),
            vmem((ne, 2, 8, half), bf16),
            vmem((peers, n, 2, 8, cw), bf16),
            vmem((peers * tokens, share), f32),
            vmem((peers, tokens, 128), f32),
            vmem((peers, 8, 128), f32),
            dma((n, 4)),
            dma((1,)),
            dma((width // hidden,)),
            dma((n, 2 * ne)),
            dma((n, 2 * ne)),
            dma((n, 4)),
            dma((n, 4)),
            dma((n, 4)),
            dma((n, 4)),
            dma((n, 3)),
            dma((n, 3)),
            dma((n, 2 * ne)),
            dma((n, 2 * ne)),
            dma((n, 2 * ne)),
            dma((n, 2 * ne)),
            dma((2, peers)),
            dma((2, peers)),
        ],
        compiler_params=pltpu.CompilerParams(
            collective_id=0, has_side_effects=True, vmem_limit_bytes=VMEM_BYTES - 1024 * 1024
        ),
        name="fused",
    )(resid, moe_gain, final_gain, router, ids, targets, lengths, questions, *weights)


def kernel_fits(sizes, *arrays):
    ne, nv, nb = sizes
    resid, w_gate, lm_head, ids = arrays[0], arrays[4], arrays[7], arrays[8]
    tokens, width = resid.shape[1:]
    hidden = w_gate.shape[2]
    share = lm_head.shape[0]
    cap = row_cap(ne, tokens, ids.shape[2])
    rows = 8 * ne * cap
    need = 2 * (3 * width * hidden + rows * (4 * width + 6 * hidden) + 8 * ne * 8 * width)
    return (
        nv == 2
        and nb == 4
        and tokens == 8
        and ids.shape[2] == 2
        and cap <= 8
        and ne * 2 * cap % 8 == 0
        and width % (2 * hidden) == 0
        and width % (2 * CHUNKS * 128) == 0
        and hidden % (width // 2 // CHUNKS) == 0
        and hidden % 256 == 0
        and share == 2 * hidden
        and ne * nv * tokens <= 128
        and need < VMEM_BYTES - 4 * 1024 * 1024
    )


def on_device_kernel(
    sizes,
    resid,
    moe_gain,
    final_gain,
    router,
    w_gate,
    w_up,
    w_down,
    lm_head,
    expert_ids,
    target_ids,
    choice_len,
    choice_question,
):
    return fused_call(
        sizes,
        resid[0],
        moe_gain.reshape(1, -1),
        final_gain.reshape(1, -1),
        router.T,
        expert_ids[0].T,
        target_ids,
        choice_len,
        choice_question,
        w_gate,
        w_up,
        w_down,
        lm_head,
    )


def either(sizes, *arrays):
    if kernel_fits(sizes, *arrays):
        return on_device_kernel(sizes, *arrays)
    return on_device(*arrays)


def solution(mesh):
    sizes = tuple(mesh.shape[axis] for axis in ("expert", "vocab", "batch"))
    return jax.shard_map(
        functools.partial(either, sizes),
        mesh=mesh,
        in_specs=(
            P("batch", ("expert", "vocab"), None),
            P(),
            P(),
            P(),
            P("expert", None, ("vocab", "batch")),
            P("expert", None, ("vocab", "batch")),
            P("expert", ("vocab", "batch"), None),
            P(("expert", "vocab"), None),
            P("batch", ("expert", "vocab"), None),
            P("batch", None),
            P("batch", None),
            P("batch", None),
        ),
        out_specs=(P("batch", ("expert", "vocab")), P("batch", None)),
        check_vma=False,
    )
```

time: 108 us -> 85.1 us (0.79)
  Pallas kernels: 99.6 us -> 82 us
  other arithmetic: 4.86 us -> 0 us
    pallas_call x2 -> x1, Pallas kernels: 99.6 us -> 82 us  [fused_call(): pl.pallas_call(functools.partial(fused_kernel, ne, nv, nb, cap), out_shap...]
    reduce_sum x6 -> x0, other arithmetic: 2.87 us -> none  [the longest x1 1.07 us: rms_scale(): mean_square = jnp.mean(values * values, axis=-1, keepdims=True)]
    unnamed x10 -> x2, local copies, waits for them, and re-layouts: 0.02 us -> 2.25 us
where the time goes in v1:
time: 85.1 us; the launch traced here: 84.9 us
  Pallas kernels  82 us (96%)
  local copies, waits for them, and re-layouts  2.25 us (3%)
    pallas_call x1, Pallas kernels, fused_call(): pl.pallas_call(functools.partial(fused_kernel, ne, nv, nb, cap), out_shap...  82 us
    unnamed x2, local copies, waits for them, and re-layouts  2.25 us

profile of v1, /device:TPU:0, one launch (start us, length us, event | category | flops | bytes accessed | tf_op | source)
XLA Modules:
  0.0 84.9 jit_solution(11171900310960158891)
XLA Ops:
  0.6 82.0 %fused.1 = (f32[1,8]{1,0:T(1,128)}, f32[1,8]{1,0:T(1,128)}) custom-call(bf16[8,6144]{1,0:T(8,128)(2,1)} %bitcast.7, f32[1,6144]{1,0:T(1,128)} %bitcast.9, f32[1,6144]{1,0:T(1,128)} %bitcast.10, bf16[4,6144]{1,0:T(4,128)(2,1)} %bitcast.8, s32[2,8]{1,0:T(2,128)} %bitcast.11, s32[1,64]{1,0:T(1,128)} %target_ref.1, s32[1,8]{1,0:T(1,128)} %length_ref.1, ...), custom_call_target="tpu_custom_call" | custom-call | tf_op jit(solution)/shard_map/fused/pallas_call | solution.py:704
  82.7 1.1 %copy.16 = f32[1,8]{1,0:T(1,128)} copy(f32[1,8]{1,0:T(1,128)} %get-tuple-element.4) | data formatting | bytes 64
  83.8 1.1 %copy.17 = f32[1,8]{1,0:T(1,128)} copy(f32[1,8]{1,0:T(1,128)} %get-tuple-element.5) | data formatting | bytes 64

commit v2 on v1

--- a/solution.py
+++ b/solution.py
@@ -173,9 +173,16 @@
     )
 
 
-SKEW_MIX = 5
-SKEW_FORWARD = 7
-SKEW_HEAD = 8
+PAIRS = CHUNKS // 2
+FIRST_ORDER = (
+    "p0", "p1", "r0", "r1", "p2", "r2", "c0", "r3", "c1", "r4", "e0", "r5", "c2", "e1", "c3", "e2",
+    "c4", "e3", "c5", "e4", "e5",
+)
+SECOND_ORDER = (
+    "d0", "d1", "d2", "s0", "d3", "s1", "d4", "s2", "d5", "s3", "a0", "a1", "s4", "s5", "a2", "b0",
+    "a3", "b1", "a4", "a5", "b2", "b3", "b4", "b5", "m0", "m1", "f0", "m2", "f1", "f2", "h0", "f3",
+    "h1", "f4", "h2", "f5", "h3", "h4", "h5",
+)
 
 
 def row_cap(ne, tokens, routes):
@@ -188,6 +195,20 @@
 
 def iota(shape, axis):
     return lax.broadcasted_iota(jnp.int32, shape, axis)
+
+
+def landed(ref, send_sem, recv_sem, partner):
+    push(ref, ref, send_sem, recv_sem, partner).wait_recv()
+
+
+def sent(ref, send_sem, recv_sem, partner):
+    push(ref, ref, send_sem, recv_sem, partner).wait_send()
+
+
+def run(order, stages):
+    for word in order:
+        with jax.named_scope(word):
+            stages[word[0]](int(word[1:]))
 
 
 def as_column(row, count):
@@ -206,6 +227,19 @@
     nv,
     nb,
     cap,
+    resid_any,
+    moe_gain_any,
+    final_gain_any,
+    router_any,
+    ids_any,
+    target_any,
+    length_any,
+    question_any,
+    wg_hbm,
+    wu_hbm,
+    wd_hbm,
+    head_hbm,
+    out_ref,
     resid_ref,
     moe_gain_ref,
     final_gain_ref,
@@ -214,12 +248,6 @@
     target_ref,
     length_ref,
     question_ref,
-    wg_hbm,
-    wu_hbm,
-    wd_hbm,
-    head_hbm,
-    logprob_ref,
-    prob_ref,
     big,
     wd,
     zout,
@@ -242,6 +270,7 @@
     logits,
     scales,
     stats,
+    i_sem,
     w_sem,
     wd_sem,
     h_sem,
@@ -257,6 +286,7 @@
     o_recv,
     y_send,
     y_recv,
+    x_recv,
     s_send,
     s_recv,
 ):
@@ -267,6 +297,8 @@
     half = width // 2
     n = CHUNKS
     cw = half // n
+    pw = 2 * cw
+    zw = pw * 5 // 8
     chip_rows = ne * 2 * cap
     tiles = chip_rows // 8
     rows = 4 * chip_rows
@@ -291,29 +323,42 @@
                 to = lax.rem(e + k, ne)
                 column.append((k * 2 + s, to, other if s else core, (to, v, turned if s else b)))
 
+    def packed(p):
+        return pl.ds(p * zw, zw)
+
+    def stacked(value, count):
+        part = value.shape[1] // count
+        return jnp.concatenate([value[:, g * part : (g + 1) * part] for g in range(count)], axis=0)
+
     def at(k):
         p = lax.rem(me + k, peers)
         return (p // nv, lax.rem(p, nv), b)
-
-    weight_loads = {}
-    for j in range(n):
-        for which, source in enumerate((wg_hbm, wu_hbm)):
-            for h in range(2):
-                first = h * half + j * cw
-                weight_loads[j, which, h] = pltpu.make_async_copy(
-                    source.at[0, pl.ds(first, cw)],
-                    big.at[pl.ds(which * width + first, cw)],
-                    w_sem.at[j, which * 2 + h],
-                )
-                weight_loads[j, which, h].start()
-    down_load = pltpu.make_async_copy(wd_hbm.at[0], wd, wd_sem.at[0])
-    down_load.start()
 
     barrier = pltpu.get_barrier_semaphore()
     greeted = [where for _, _, _, where in column]
     greeted += [(lax.rem(e + k, ne), 1 - v, b) for k in range(ne)] + [along]
     for partner in greeted:
         pl.semaphore_signal(barrier, inc=1, device_id=partner, device_id_type=MESH)
+
+    input_loads = [
+        pltpu.make_async_copy(source, target, i_sem.at[i])
+        for i, (source, target) in enumerate(
+            (
+                (resid_any, resid_ref),
+                (moe_gain_any, moe_gain_ref),
+                (ids_any, ids_ref),
+                (router_any, router_ref),
+                (final_gain_any, final_gain_ref),
+                (target_any, target_ref),
+                (length_any, length_ref),
+                (question_any, question_ref),
+            )
+        )
+    ]
+    for load in input_loads:
+        load.start()
+    for load in input_loads[:3]:
+        load.wait()
 
     stream = wide(resid_ref[...])
     mean_square = jnp.sum(stream * stream, axis=1, keepdims=True) * (1.0 / width)
@@ -321,36 +366,60 @@
     ids = wide(ids_ref[...])
     first_row, second_row = ids[0:1, :], ids[1:2, :]
     expert_of = wide(lax.shift_right_logical(iota((ne * 8, tokens), 0), 3))
-    slot_of = wide(iota((ne * 8, tokens), 0) & 7)
+    line_of = iota((ne * 8, tokens), 0) & 7
     named = (first_row == expert_of) | (second_row == expert_of)
     before = jnp.where(iota((tokens, tokens), 0) < iota((tokens, tokens), 1), 1.0, 0.0)
     rank = jnp.dot(jnp.where(named, 1.0, 0.0), before, preferred_element_type=jnp.float32)
-    dispatch = jnp.where(named & (rank == slot_of), 1.0, 0.0)
-    for h in range(2):
-        for j in range(n):
-            first = h * half + j * cw
-            routed = jnp.dot(
-                dispatch, normed[:, first : first + cw], preferred_element_type=jnp.float32
+    four = jnp.where(named & (rank == wide(line_of & 3)), 1.0, 0.0)
+    fifth = jnp.where(named & (rank == 4.0), 1.0, 0.0)
+    pick_four = jnp.concatenate(
+        [jnp.where(line_of < 4, four, 0.0), jnp.where(line_of < 4, 0.0, four)], axis=1
+    )
+    pick_fifth = jnp.concatenate([jnp.where(line_of == g, fifth, 0.0) for g in range(8)], axis=1)
+
+    def product(left, right):
+        return jnp.dot(left, right, preferred_element_type=jnp.float32)
+
+    for p in range(PAIRS):
+        for h in range(2):
+            piece = normed[:, h * half + p * pw : h * half + (p + 1) * pw]
+            zout[h, :, :, p * zw : p * zw + cw] = (
+                product(pick_four, stacked(piece, 2)).reshape(ne, 8, cw).astype(bf16)
             )
-            zout[h, :, :, cols(j)] = routed.reshape(ne, 8, cw).astype(bf16)
+            zout[h, :, :, p * zw + cw : (p + 1) * zw] = (
+                product(pick_fifth, stacked(piece, 8)).reshape(ne, 8, zw - cw).astype(bf16)
+            )
     pl.semaphore_wait(barrier, len(greeted))
 
     z_copies = {}
-    for j in range(n):
+    for p in range(PAIRS):
         for slot, to, ct, where in column:
-            z_copies[j, slot] = push(
-                zout.at[ct, to, :, cols(j)],
-                zin.at[e, core, :, cols(j)],
-                z_send.at[j, slot],
-                z_recv.at[j, slot],
+            z_copies[p, slot] = push(
+                zout.at[ct, to, :, packed(p)],
+                zin.at[e * 2 + core, :, packed(p)],
+                z_send.at[0],
+                z_recv.at[p],
                 where,
             )
-            z_copies[j, slot].start()
-    zin[e, core] = zout[core, e]
-
+            z_copies[p, slot].start()
+    zin[e * 2 + core] = zout[core, e]
+
+    for j in range(n):
+        for which, source in enumerate((wg_hbm, wu_hbm)):
+            for h in range(2):
+                first = h * half + j * cw
+                pltpu.make_async_copy(
+                    source.at[0, pl.ds(first, cw)],
+                    big.at[pl.ds(which * width + first, cw)],
+                    w_sem.at[j],
+                ).start()
+    down_load = pltpu.make_async_copy(wd_hbm.at[0], wd, wd_sem.at[0])
+    down_load.start()
+    for load in input_loads[3:]:
+        load.wait()
     first_id, second_id = as_column(first_row, tokens), as_column(second_row, tokens)
     expert_lane = wide(lax.shift_right_logical(iota((tokens, ne * 8), 1), 3))
-    slot_lane = wide(iota((tokens, ne * 8), 1) & 7)
+    line_lane = iota((tokens, ne * 8), 1) & 7
     first_here, second_here = first_id == expert_lane, second_id == expert_lane
     after = jnp.where(iota((tokens, tokens), 1) < iota((tokens, tokens), 0), 1.0, 0.0)
     rank = jnp.dot(
@@ -364,29 +433,42 @@
         second_logit = second_logit + jnp.where(second_id == k, router_logit, 0.0)
     first_gate = 1.0 / (1.0 + jnp.exp(second_logit - first_logit))
     second_gate = 1.0 / (1.0 + jnp.exp(first_logit - second_logit))
-    combine = jnp.where(
-        rank == slot_lane,
-        jnp.where(first_here, first_gate, jnp.where(second_here, second_gate, 0.0)),
-        0.0,
-    )
-    coarse = wide(combine.astype(bf16))
-    combine = jnp.concatenate([coarse, combine - coarse], axis=0).astype(bf16)
-
-    def packing(shape, packed_axis):
-        padded = iota(shape, 1 - packed_axis)
-        slot = padded & 7
-        place = lax.shift_right_logical(padded, 3) * cap + slot
-        return jnp.where((slot < cap) & (place == iota(shape, packed_axis)), 1.0, 0.0).astype(bf16)
-
-    pack = packing((chip_rows, ne * 16), 0)
-    unpack = packing((ne * 16, chip_rows), 1)
+    gate = jnp.where(first_here, first_gate, jnp.where(second_here, second_gate, 0.0))
+    four = jnp.where(rank == wide(line_lane & 3), gate, 0.0)
+    fifth = jnp.where(rank == 4.0, gate, 0.0)
+
+    def two_terms(weights):
+        weights = jnp.concatenate(weights, axis=0)
+        coarse = wide(weights.astype(bf16))
+        return jnp.concatenate([coarse, weights - coarse], axis=0).astype(bf16)
+
+    mix_four = two_terms([jnp.where(line_lane < 4, four, 0.0), jnp.where(line_lane < 4, 0.0, four)])
+    mix_fifth = two_terms([jnp.where(line_lane == g, fifth, 0.0) for g in range(8)])
+
+    sources = 2 * ne
+    moved = (sources * 8, sources * 8)
+
+    def four_place(axis):
+        index = iota(moved, axis)
+        side = jnp.where(index < sources * 4, 0, 1)
+        within = index - side * (sources * 4)
+        target = lax.shift_right_logical(within, 2) * 8 + side * 4 + (within & 3)
+        return jnp.where(target == iota(moved, 1 - axis), 1.0, 0.0).astype(bf16)
+
+    def fifth_place(axis):
+        index, target = iota(moved, axis), iota(moved, 1 - axis)
+        fits = ((target & 7) * sources + lax.shift_right_logical(target, 3)) == index
+        return jnp.where(fits, 1.0, 0.0).astype(bf16)
+
+    open_four, open_fifth = four_place(0), fifth_place(0)
+    close_four, close_fifth = four_place(1), fifth_place(1)
 
     def plane_push(src_slot, dst_slot, j, partner):
         return push(
             xs.at[src_slot, core, :, :, cols(j)],
             xs.at[dst_slot, core, :, :, cols(j)],
-            c_send.at[j, dst_slot],
-            c_recv.at[j, dst_slot],
+            c_send.at[0],
+            c_recv.at[j, dst_slot - 1],
             partner,
         )
 
@@ -396,22 +478,32 @@
         m_copies[j, slot] = push(
             xs.at[slot, core, :, :, cols(j)],
             xs.at[slot, core, :, :, cols(j)],
-            m_send.at[j, slot],
-            m_recv.at[j, slot],
+            m_send.at[0],
+            m_recv.at[j],
             mate,
         )
         m_copies[j, slot].start()
 
-    def pack_rows(j):
-        for slot, _, _, _ in column:
-            z_copies[j, slot].wait_recv()
-        padded = wide(zin[:, :, :, cols(j)]).reshape(ne * 16, cw).astype(bf16)
-        packed = jnp.dot(pack, padded, preferred_element_type=jnp.float32)
-        xs[0, core, :, :, cols(j)] = packed.reshape(tiles, 8, cw).astype(bf16)
-        for slot, partner in ((1, across), (2, along)):
-            c_copies[j, slot] = plane_push(0, slot, j, partner)
-            c_copies[j, slot].start()
-        mate_push(0, j)
+    def open_pair(p):
+        landed(zin.at[: sources - 1, :, packed(p)], z_send.at[0], z_recv.at[p], mate)
+        block_rows = wide(zin[:, :, packed(p)])
+        fours = product(
+            open_four, block_rows[:, :, :cw].reshape(sources * 8, cw).astype(bf16)
+        ).reshape(2, ne, 8, cw)
+        fifths = product(
+            open_fifth, block_rows[:, :, cw:].reshape(sources * 8, zw - cw).astype(bf16)
+        )
+        for side in range(2):
+            j = 2 * p + side
+            xs[0, core, 0:ne, :, cols(j)] = fours[side].astype(bf16)
+            row = [
+                fifths[g * sources : (g + 1) * sources] for g in range(side * 4, side * 4 + 4)
+            ]
+            xs[0, core, ne, :, cols(j)] = jnp.concatenate(row, axis=1).astype(bf16)
+            for slot, partner in ((1, across), (2, along)):
+                c_copies[j, slot] = plane_push(0, slot, j, partner)
+                c_copies[j, slot].start()
+            mate_push(0, j)
 
     def relay(j):
         source, partner = (1, along) if j % 2 == 0 else (2, across)
@@ -429,29 +521,23 @@
     tile = min(256, hidden)
 
     def expand(j):
-        for slot in range(4):
-            m_copies[j, slot].wait_recv()
+        landed(xs.at[:, other, :, :, cols(j)], m_send.at[0], m_recv.at[j], mate)
         for h in range(2):
             xl[h] = wide(xs[:, h, :, :, cols(j)]).reshape(rows, cw).astype(bf16)
-        for which in range(2):
-            for h in range(2):
-                weight_loads[j, which, h].wait()
-
-        @pl.loop(0, hidden // tile)
-        def _(i):
-            where = pl.ds(pl.multiple_of(i * tile, tile), tile)
-
-            def product(which):
+        pltpu.make_async_copy(
+            head_hbm.at[pl.ds(0, 4 * cw), pl.ds(0, hidden)], big.at[pl.ds(0, 4 * cw)], w_sem.at[j]
+        ).wait()
+
+        for i in range(hidden // tile):
+            where = pl.ds(i * tile, tile)
+
+            def raw(which):
                 low = which * width + j * cw
-                return jnp.dot(
-                    xl[0], big[low : low + cw, where], preferred_element_type=jnp.float32
-                ) + jnp.dot(
-                    xl[1],
-                    big[low + half : low + half + cw, where],
-                    preferred_element_type=jnp.float32,
+                return product(xl[0], big[low : low + cw, where]) + product(
+                    xl[1], big[low + half : low + half + cw, where]
                 )
 
-            g, u = product(0), product(1)
+            g, u = raw(0), raw(1)
             if j > 0:
                 g, u = g + g_acc[:, where], u + u_acc[:, where]
             if j < n - 1:
@@ -460,10 +546,7 @@
             else:
                 hid[:, where] = (g / (1.0 + jnp.exp(-g)) * u).astype(bf16)
 
-    for i in range(n + 3):
-        for skew, stage in enumerate((pack_rows, relay, corner, expand)):
-            if 0 <= i - skew < n:
-                stage(i - skew)
+    run(FIRST_ORDER, {"p": open_pair, "r": relay, "c": corner, "e": expand})
 
     head_loads = []
     per_half = half // block
@@ -483,93 +566,111 @@
     rp, yc, xc, zc, gz, gx = {}, {}, {}, {}, {}, {}
 
     def down(j):
-        def product(side):
+        def part(side):
             where = pl.ds(pl.multiple_of(side * half + j * cw, 128), cw)
-            return jnp.dot(hid[...], wd[:, where], preferred_element_type=jnp.float32)
-
-        pm[:, :, :, cols(j)] = product(other).reshape(4, tiles, 8, cw).astype(bf16)
+            return product(hid[...], wd[:, where])
+
+        pm[:, :, :, cols(j)] = part(other).reshape(4, tiles, 8, cw).astype(bf16)
         rp[j] = push(
-            pm.at[:, :, :, cols(j)], rpair.at[:, :, :, cols(j)], r_send.at[j, 0], r_recv.at[j, 0], mate
+            pm.at[:, :, :, cols(j)], rpair.at[:, :, :, cols(j)], r_send.at[0], r_recv.at[j, 0], mate
         )
         rp[j].start()
-        po[:, cols(j)] = product(core)
+        po[:, :, cols(j)] = part(core).reshape(4, chip_rows, cw)
 
     def pair_sum(j):
         rp[j].wait_recv()
-        total = po[:, cols(j)] + wide(rpair[:, :, :, cols(j)]).reshape(rows, cw)
-        sy[:, :, :, cols(j)] = total[2 * chip_rows :].reshape(2, tiles, 8, cw).astype(bf16)
+        total = po[:, :, cols(j)] + wide(rpair[:, :, :, cols(j)]).reshape(4, chip_rows, cw)
+        kept, passed, partner = ((0, 1), (2, 3), along) if j % 2 == 0 else ((0, 2), (1, 3), across)
+        for i in range(2):
+            sy[i, :, :, cols(j)] = total[passed[i]].reshape(tiles, 8, cw).astype(bf16)
         yc[j] = push(
-            sy.at[:, :, :, cols(j)], ry.at[:, :, :, cols(j)], r_send.at[j, 1], r_recv.at[j, 1], along
+            sy.at[:, :, :, cols(j)], ry.at[:, :, :, cols(j)], r_send.at[1], r_recv.at[j, 1], partner
         )
         yc[j].start()
-        po[0 : 2 * chip_rows, cols(j)] = total[: 2 * chip_rows]
-
-    def y_sum(j):
+        for i in range(2):
+            po[i, :, cols(j)] = total[kept[i]]
+
+    def side_sum(j):
         yc[j].wait_recv()
-        total = po[0 : 2 * chip_rows, cols(j)] + wide(ry[:, :, :, cols(j)]).reshape(2 * chip_rows, cw)
-        sx[:, :, cols(j)] = total[chip_rows:].reshape(tiles, 8, cw).astype(bf16)
+        total = po[1, :, cols(j)] + wide(ry[1, :, :, cols(j)]).reshape(chip_rows, cw)
+        sx[:, :, cols(j)] = total.reshape(tiles, 8, cw).astype(bf16)
+        partner = across if j % 2 == 0 else along
         xc[j] = push(
-            sx.at[:, :, cols(j)], rx.at[:, :, cols(j)], r_send.at[j, 2], r_recv.at[j, 2], across
+            sx.at[:, :, cols(j)], rx.at[:, :, cols(j)], r_send.at[2], r_recv.at[j, 2], partner
         )
         xc[j].start()
-        po[0:chip_rows, cols(j)] = total[:chip_rows]
-
-    def x_sum(j):
+        po[0, :, cols(j)] = po[0, :, cols(j)] + wide(ry[0, :, :, cols(j)]).reshape(chip_rows, cw)
+
+    def own_sum(j):
         xc[j].wait_recv()
-        total = po[0:chip_rows, cols(j)] + wide(rx[:, :, cols(j)]).reshape(chip_rows, cw)
-        padded = jnp.dot(unpack, total.astype(bf16), preferred_element_type=jnp.float32)
-        zs[:, :, :, cols(j)] = padded.reshape(ne, 2, 8, cw).astype(bf16)
+        po[0, :, cols(j)] = po[0, :, cols(j)] + wide(rx[:, :, cols(j)]).reshape(chip_rows, cw)
+        if j % 2 == 0:
+            return
+        p = j // 2
+        total = po[0, :, p * pw : (p + 1) * pw]
+        fours = product(close_four, stacked(total[: sources * 4], 2).astype(bf16))
+        fifths = product(close_fifth, stacked(total[sources * 4 :], 8).astype(bf16))
+        zs[:, :, :, p * zw : p * zw + cw] = fours.reshape(ne, 2, 8, cw).astype(bf16)
+        zs[:, :, :, p * zw + cw : (p + 1) * zw] = fifths.reshape(ne, 2, 8, zw - cw).astype(bf16)
         for slot, to, ct, where in column:
-            zc[j, slot] = push(
-                zs.at[to, ct, :, cols(j)],
-                zo.at[e, core, :, cols(j)],
-                o_send.at[j, slot],
-                o_recv.at[j, slot],
+            zc[p, slot] = push(
+                zs.at[to, ct, :, packed(p)],
+                zo.at[e * 2 + core, :, packed(p)],
+                o_send.at[0],
+                o_recv.at[p],
                 where,
             )
-            zc[j, slot].start()
-        zo[e, core, :, cols(j)] = zs[e, core, :, cols(j)]
+            zc[p, slot].start()
+        zo[e * 2 + core, :, packed(p)] = zs[e, core, :, packed(p)]
 
     squares = [jnp.zeros((tokens, 1), jnp.float32)]
 
-    def mix(j):
-        for slot, _, _, _ in column:
-            zc[j, slot].wait_recv()
+    def mix(p):
+        landed(zo.at[: sources - 1, :, packed(p)], o_send.at[0], o_recv.at[p], mate)
+        every = wide(zo[:, :, packed(p)]).reshape(ne, 2, 8, zw)
         for h in range(2):
-            first = h * half + j * cw
-            returned = wide(zo[:, h, :, cols(j)]).reshape(ne * 8, cw).astype(bf16)
-            weighted = jnp.dot(combine, returned, preferred_element_type=jnp.float32)
-            mixed = wide(resid_ref[:, first : first + cw]) + (weighted[:tokens] + weighted[tokens:])
-            squares[0] = squares[0] + jnp.sum(mixed * mixed, axis=1, keepdims=True)
-            ys[me, j, h] = (mixed * final_gain_ref[:, first : first + cw]).astype(bf16)
-        for k in range(1, ne):
-            gz[j, k] = push(
-                ys.at[me, j],
-                ys.at[me, j],
-                y_send.at[j, k],
-                y_recv.at[j, k],
-                (lax.rem(e + k, ne), v, b),
-            )
-            gz[j, k].start()
-        turn(j, 0)
+            fours = product(mix_four, every[:, h, :, :cw].reshape(ne * 8, cw).astype(bf16))
+            fours = fours[: 2 * tokens] + fours[2 * tokens :]
+            fifths = product(mix_fifth, every[:, h, :, cw:].reshape(ne * 8, zw - cw).astype(bf16))
+            fifths = fifths[: 8 * tokens] + fifths[8 * tokens :]
+            for side in range(2):
+                j = 2 * p + side
+                first = h * half + j * cw
+                row = [fifths[g * tokens : (g + 1) * tokens] for g in range(side * 4, side * 4 + 4)]
+                weighted = fours[side * tokens : (side + 1) * tokens] + jnp.concatenate(row, axis=1)
+                mixed = wide(resid_ref[:, first : first + cw]) + weighted
+                squares[0] = squares[0] + jnp.sum(mixed * mixed, axis=1, keepdims=True)
+                ys[me, j, h] = (mixed * final_gain_ref[:, first : first + cw]).astype(bf16)
+        for j in (2 * p, 2 * p + 1):
+            for k in range(1, ne):
+                gz[j, k] = push(
+                    ys.at[me, j],
+                    ys.at[me, j],
+                    y_send.at[0],
+                    y_recv.at[j, k - 1],
+                    (lax.rem(e + k, ne), v, b),
+                )
+                gz[j, k].start()
+            turn(j, 0)
+        if p == PAIRS - 1:
+            share_scale()
 
     def turn(j, k):
         slot = lax.rem(e + ne - k, ne) * nv + v
         gx[j, k] = push(
-            ys.at[slot, j], ys.at[slot, j], y_send.at[j, ne + k], y_recv.at[j, ne + k], across
+            ys.at[slot, j], ys.at[slot, j], y_send.at[1], x_recv.at[j], across
         )
         gx[j, k].start()
 
     def forward(j):
-        for k in (1, 3, 2) if ne == 4 else range(1, ne):
+        for k in (1, 3, 2):
             gz[j, k].wait_recv()
             turn(j, k)
 
     head_tile = min(256, share)
 
     def head(j):
-        for k in range(ne):
-            gx[j, k].wait_recv()
+        landed(ys.at[:ne, j], y_send.at[1], x_recv.at[j], across)
         if (j * cw) % block == 0:
             for h in range(2):
                 head_loads[(j * cw) // block * 2 + h].wait()
@@ -579,9 +680,8 @@
         left = (j * cw) % block
         low = (j * cw) // block * share
 
-        @pl.loop(0, share // head_tile)
-        def _(i):
-            first = pl.multiple_of(i * head_tile, head_tile)
+        for i in range(share // head_tile):
+            first = i * head_tile
             found = 0.0
             for h in range(2):
                 found = found + lax.dot_general(
@@ -596,34 +696,29 @@
 
     small = []
 
-    def share_scale(j):
-        if j < n - 1:
-            return
+    def share_scale():
         scale = lax.rsqrt(squares[0] * (1.0 / width) + epsilon)
         scales[me] = jnp.broadcast_to(scale, (tokens, 128))
         for k in range(1, peers):
             small.append(
-                push(scales.at[me], scales.at[me], s_send.at[0, k], s_recv.at[0, k], at(k))
+                push(scales.at[me], scales.at[me], s_send.at[0], s_recv.at[0], at(k))
             )
             small[-1].start()
 
-    stages = (
-        (0, down),
-        (1, pair_sum),
-        (2, y_sum),
-        (3, x_sum),
-        (SKEW_MIX, mix),
-        (SKEW_MIX, share_scale),
-        (SKEW_FORWARD, forward),
-        (SKEW_HEAD, head),
-    )
-    for i in range(n + SKEW_HEAD):
-        for skew, stage in stages:
-            if 0 <= i - skew < n:
-                stage(i - skew)
-
-    for copy in small:
-        copy.wait_recv()
+    run(
+        SECOND_ORDER,
+        {
+            "d": down,
+            "s": pair_sum,
+            "a": side_sum,
+            "b": own_sum,
+            "m": mix,
+            "f": forward,
+            "h": head,
+        },
+    )
+
+    landed(scales.at[: peers - 1], s_send.at[0], s_recv.at[0], mate)
     group = peers * tokens
     lanes = 128
     scaled = logits[...] * scales[...].reshape(group, lanes)[:, 0:1]
@@ -639,7 +734,7 @@
         jnp.where(line == 1, as_row(total, lanes), jnp.where(line == 2, as_row(hit, lanes), 0.0)),
     )
     sends = [
-        push(stats.at[me], stats.at[me], s_send.at[1, k], s_recv.at[1, k], at(k))
+        push(stats.at[me], stats.at[me], s_send.at[1], s_recv.at[1], at(k))
         for k in range(1, peers)
     ]
     for copy in sends:
@@ -654,8 +749,7 @@
     member = (place >= ends - lengths) & (place < ends)
     same = questions == questions_row
 
-    for copy in sends:
-        copy.wait_recv()
+    landed(stats.at[: peers - 1], s_send.at[1], s_recv.at[1], mate)
     every = stats[...]
     best = jnp.max(every[:, 0:1, :], axis=0)
     summed = jnp.sum(every[:, 1:2, :] * jnp.exp(every[:, 0:1, :] - best[None]), axis=0)
@@ -667,20 +761,31 @@
         axis=1,
         keepdims=True,
     )
-    logprob_ref[...] = as_row(own, tokens)
+    found = as_row(own, lanes)
     average = jnp.sum(jnp.where(member, logprob, 0.0), axis=1, keepdims=True) / lengths
     question_top = jnp.max(
         jnp.where(same, as_row(average, choices), -jnp.inf), axis=1, keepdims=True
     )
     raised = jnp.exp(average - question_top)
     denominator = jnp.sum(jnp.where(same, as_row(raised, choices), 0.0), axis=1, keepdims=True)
-    prob_ref[...] = as_row(raised / denominator, choices)
-
-    for copies in (z_copies, c_copies, m_copies, rp, yc, xc, zc, gz, gx):
-        for copy in copies.values():
-            copy.wait_send()
-    for copy in small + sends:
-        copy.wait_send()
+    prob = raised / denominator
+    far = iota((choices, lanes), 1) == iota((choices, lanes), 0) + tokens
+    out_ref[...] = found + jnp.sum(jnp.where(far, prob, 0.0), axis=0, keepdims=True)
+
+    for ref, send, recv in (
+        (zin.at[: 2 * ne - 1], z_send.at[0], z_recv.at[0]),
+        (xs.at[:3, 0], c_send.at[0], c_recv.at[0, 0]),
+        (xs.at[:, 0], m_send.at[0], m_recv.at[0]),
+        (pm, r_send.at[0], r_recv.at[0, 0]),
+        (sy, r_send.at[1], r_recv.at[0, 1]),
+        (sx, r_send.at[2], r_recv.at[0, 2]),
+        (zo.at[: 2 * ne - 1], o_send.at[0], o_recv.at[0]),
+        (ys.at[: ne - 1], y_send.at[0], y_recv.at[0, 0]),
+        (ys.at[:ne], y_send.at[1], x_recv.at[0]),
+        (scales.at[: peers - 1], s_send.at[0], s_recv.at[0]),
+        (stats.at[: peers - 1], s_send.at[1], s_recv.at[1]),
+    ):
+        sent(ref, send, recv, mate)
 
 
 def fused_call(sizes, resid, moe_gain, final_gain, router, ids, targets, lengths, questions, *weights):
@@ -696,6 +801,7 @@
     peers = ne * nv
     n = CHUNKS
     cw = half // n
+    zw = half * 5 // 8
     bf16, f32 = jnp.bfloat16, jnp.float32
     dma = pltpu.SemaphoreType.DMA
     vmem = pltpu.VMEM
@@ -703,52 +809,59 @@
     anywhere = pl.BlockSpec(memory_space=pl.ANY)
     return pl.pallas_call(
         functools.partial(fused_kernel, ne, nv, nb, cap),
-        out_shape=(
-            jax.ShapeDtypeStruct((1, tokens), f32),
-            jax.ShapeDtypeStruct((1, lengths.shape[1]), f32),
-        ),
-        in_specs=[vm] * 8 + [anywhere] * 4,
-        out_specs=(vm, vm),
+        out_shape=pltpu.VMEM((1, 128), f32),
+        in_specs=[anywhere] * 12,
+        out_specs=vm,
         scratch_shapes=[
+            vmem(resid.shape, bf16),
+            vmem(moe_gain.shape, f32),
+            vmem(final_gain.shape, f32),
+            vmem(router.shape, bf16),
+            vmem(ids.shape, jnp.int32),
+            vmem(targets.shape, jnp.int32),
+            vmem(lengths.shape, jnp.int32),
+            vmem(questions.shape, jnp.int32),
             vmem((2 * width, hidden), bf16),
             vmem((hidden, width), bf16),
-            vmem((2, ne, 8, half), bf16),
-            vmem((ne, 2, 8, half), bf16),
+            vmem((2, ne, 8, zw), bf16),
+            vmem((2 * ne, 8, zw), bf16),
             vmem((4, 2, tiles, 8, half), bf16),
             vmem((2, rows, cw), bf16),
             vmem((rows, hidden), f32),
             vmem((rows, hidden), f32),
             vmem((rows, hidden), bf16),
             vmem((4, tiles, 8, half), bf16),
-            vmem((rows, half), f32),
+            vmem((4, tiles * 8, half), f32),
             vmem((4, tiles, 8, half), bf16),
             vmem((2, tiles, 8, half), bf16),
             vmem((2, tiles, 8, half), bf16),
             vmem((tiles, 8, half), bf16),
             vmem((tiles, 8, half), bf16),
-            vmem((ne, 2, 8, half), bf16),
-            vmem((ne, 2, 8, half), bf16),
+            vmem((ne, 2, 8, zw), bf16),
+            vmem((2 * ne, 8, zw), bf16),
             vmem((peers, n, 2, 8, cw), bf16),
             vmem((peers * tokens, share), f32),
             vmem((peers, tokens, 128), f32),
             vmem((peers, 8, 128), f32),
-            dma((n, 4)),
+            dma((8,)),
+            dma((n,)),
             dma((1,)),
             dma((width // hidden,)),
-            dma((n, 2 * ne)),
-            dma((n, 2 * ne)),
-            dma((n, 4)),
-            dma((n, 4)),
-            dma((n, 4)),
-            dma((n, 4)),
+            dma((1,)),
+            dma((PAIRS,)),
+            dma((1,)),
             dma((n, 3)),
+            dma((1,)),
+            dma((n,)),
+            dma((3,)),
             dma((n, 3)),
-            dma((n, 2 * ne)),
-            dma((n, 2 * ne)),
-            dma((n, 2 * ne)),
-            dma((n, 2 * ne)),
-            dma((2, peers)),
-            dma((2, peers)),
+            dma((1,)),
+            dma((PAIRS,)),
+            dma((2,)),
+            dma((n, 3)),
+            dma((n,)),
+            dma((2,)),
+            dma((2,)),
         ],
         compiler_params=pltpu.CompilerParams(
             collective_id=0, has_side_effects=True, vmem_limit_bytes=VMEM_BYTES - 1024 * 1024
@@ -767,14 +880,15 @@
     rows = 8 * ne * cap
     need = 2 * (3 * width * hidden + rows * (4 * width + 6 * hidden) + 8 * ne * 8 * width)
     return (
-        nv == 2
+        ne == 4
+        and nv == 2
         and nb == 4
         and tokens == 8
         and ids.shape[2] == 2
-        and cap <= 8
+        and cap == 5
         and ne * 2 * cap % 8 == 0
         and width % (2 * hidden) == 0
-        and width % (2 * CHUNKS * 128) == 0
+        and width % (2 * CHUNKS * 512) == 0
         and hidden % (width // 2 // CHUNKS) == 0
         and hidden % 256 == 0
         and share == 2 * hidden
@@ -798,7 +912,7 @@
     choice_len,
     choice_question,
 ):
-    return fused_call(
+    found = fused_call(
         sizes,
         resid[0],
         moe_gain.reshape(1, -1),
@@ -813,6 +927,8 @@
         w_down,
         lm_head,
     )
+    tokens = resid.shape[1]
+    return found[:, :tokens], found[:, tokens : tokens + choice_len.shape[1]]
 
 
 def either(sizes, *arrays):

time: 85.1 us -> 64.8 us (0.76)
  Pallas kernels: 82 us -> 63.5 us
  local copies, waits for them, and re-layouts: 2.25 us -> 0.58 us
    pallas_call x1, Pallas kernels: 82 us -> 63.5 us  [fused_call(): pl.pallas_call(functools.partial(fused_kernel, ne, nv, nb, cap), out_shap...]
    unnamed x2 -> x0, local copies, waits for them, and re-layouts: 2.25 us -> none
where the time goes in v2:
time: 64.8 us; the launch traced here: 64.7 us
  Pallas kernels  63.5 us (98%)
    pallas_call x1, Pallas kernels, fused_call(): pl.pallas_call(functools.partial(fused_kernel, ne, nv, nb, cap), out_shap...  63.5 us

profile of v2, /device:TPU:0, one launch (start us, length us, event | category | flops | bytes accessed | tf_op | source)
XLA Modules:
  0.0 64.7 jit_solution(6677299415688387807)
XLA Ops:
  0.6 63.5 %fused.1 = f32[1,128]{1,0:T(1,128)S(1)} custom-call(bf16[8,6144]{1,0:T(8,128)(2,1)} %bitcast.7, f32[1,6144]{1,0:T(1,128)} %bitcast.9, f32[1,6144]{1,0:T(1,128)} %bitcast.10, bf16[4,6144]{1,0:T(4,128)(2,1)} %bitcast.8, s32[2,8]{1,0:T(2,128)} %bitcast.11, s32[1,64]{1,0:T(1,128)} %target_any.1, s32[1,8]{1,0:T(1,128)} %length_any.1, s32[1,8]{1,0:T(1,128)} %question_any.1, ...), custom_call_target="tpu_custom_call" | custom-call | tf_op jit(solution)/shard_map/fused/pallas_call | solution.py:810
  64.1 0.6 fusion

commit v3 on v2

--- a/solution.py
+++ b/solution.py
@@ -643,14 +643,18 @@
                 ys[me, j, h] = (mixed * final_gain_ref[:, first : first + cw]).astype(bf16)
         for j in (2 * p, 2 * p + 1):
             for k in range(1, ne):
+                near_only = j < n - 2 and k != 2
                 gz[j, k] = push(
                     ys.at[me, j],
                     ys.at[me, j],
-                    y_send.at[0],
+                    y_send.at[2 if near_only else 0],
                     y_recv.at[j, k - 1],
                     (lax.rem(e + k, ne), v, b),
                 )
-                gz[j, k].start()
+                if near_only:
+                    pl.when(e != (ne - 1 if k == 1 else 0))(gz[j, k].start)
+                else:
+                    gz[j, k].start()
             turn(j, 0)
         if p == PAIRS - 1:
             share_scale()
@@ -664,7 +668,17 @@
 
     def forward(j):
         for k in (1, 3, 2):
-            gz[j, k].wait_recv()
+            landed(ys.at[me, j], y_send.at[0], y_recv.at[j, k - 1], mate)
+            if k == 2 and j < n - 2:
+                slot = lax.rem(e + 2, ne) * nv + v
+                onward = push(
+                    ys.at[slot, j],
+                    ys.at[slot, j],
+                    y_send.at[2],
+                    y_recv.at[j, 2 - 2 * lax.rem(e, 2)],
+                    (lax.rem(3 * e + 1, ne), v, b),
+                )
+                pl.when((e > 0) & (e < ne - 1))(onward.start)
             turn(j, k)
 
     head_tile = min(256, share)
@@ -780,12 +794,20 @@
         (sy, r_send.at[1], r_recv.at[0, 1]),
         (sx, r_send.at[2], r_recv.at[0, 2]),
         (zo.at[: 2 * ne - 1], o_send.at[0], o_recv.at[0]),
-        (ys.at[: ne - 1], y_send.at[0], y_recv.at[0, 0]),
+        (ys.at[:2, : n - 1], y_send.at[0], y_recv.at[0, 0]),
         (ys.at[:ne], y_send.at[1], x_recv.at[0]),
         (scales.at[: peers - 1], s_send.at[0], s_recv.at[0]),
         (stats.at[: peers - 1], s_send.at[1], s_recv.at[1]),
     ):
         sent(ref, send, recv, mate)
+
+    @pl.when((e > 0) & (e < ne - 1))
+    def _():
+        sent(ys.at[:2], y_send.at[2], y_recv.at[0, 0], mate)
+
+    @pl.when((e == 0) | (e == ne - 1))
+    def _():
+        sent(ys.at[0, : n - 2], y_send.at[2], y_recv.at[0, 0], mate)
 
 
 def fused_call(sizes, resid, moe_gain, final_gain, router, ids, targets, lengths, questions, *weights):
@@ -857,7 +879,7 @@
             dma((n, 3)),
             dma((1,)),
             dma((PAIRS,)),
-            dma((2,)),
+            dma((3,)),
             dma((n, 3)),
             dma((n,)),
             dma((2,)),
@@ -892,6 +914,7 @@
         and hidden % (width // 2 // CHUNKS) == 0
         and hidden % 256 == 0
         and share == 2 * hidden
+        and CHUNKS == 6
         and ne * nv * tokens <= 128
         and need < VMEM_BYTES - 4 * 1024 * 1024
     )

time: 64.8 us -> 64.9 us (level)
  no operation moved by 1% of the time
where the time goes in v3:
time: 64.9 us; the launch traced here: 64.8 us
  Pallas kernels  63.5 us (98%)
    pallas_call x1, Pallas kernels, fused_call(): pl.pallas_call(functools.partial(fused_kernel, ne, nv, nb, cap), out_shap...  63.5 us

profile of v3, /device:TPU:0, one launch (start us, length us, event | category | flops | bytes accessed | tf_op | source)
XLA Modules:
  0.0 64.8 jit_solution(3644242599468863922)
XLA Ops:
  0.6 63.5 %fused.1 = f32[1,128]{1,0:T(1,128)S(1)} custom-call(bf16[8,6144]{1,0:T(8,128)(2,1)} %bitcast.7, f32[1,6144]{1,0:T(1,128)} %bitcast.9, f32[1,6144]{1,0:T(1,128)} %bitcast.10, bf16[4,6144]{1,0:T(4,128)(2,1)} %bitcast.8, s32[2,8]{1,0:T(2,128)} %bitcast.11, s32[1,64]{1,0:T(1,128)} %target_any.1, s32[1,8]{1,0:T(1,128)} %length_any.1, s32[1,8]{1,0:T(1,128)} %question_any.1, ...), custom_call_target="tpu_custom_call" | custom-call | tf_op jit(solution)/shard_map/fused/pallas_call | solution.py:832
  64.2 0.6 fusion
